TPU v7x, 64 devices: a 2x2x8 block of a 4x4x8 slice. The times are simulated.
64 devices in a mesh: dp: 4 (over x, y), ep: 16 (over z, core).
Axes of the slice: x: 2, y: 2, z: 8, core: 2. Of those that a mesh axis runs over, the one named last changes fastest.
The devices are a block of a 4x4x8 slice.
Arguments:
- act_in: bfloat16 [8192, 2048], P(('dp', 'ep')), parts along dimension 0
- router_w: bfloat16 [2048, 64], replicated
- expert_ids: int32 [8192, 8], P(('dp', 'ep')), parts along dimension 0
- w_gate: bfloat16 [64, 2048, 1024], P('ep')
- w_up: bfloat16 [64, 2048, 1024], P('ep')
- w_down: bfloat16 [64, 1024, 2048], P('ep')
Outputs:
- output: bfloat16 [8192, 2048], P(('dp', 'ep')), parts along dimension 0
There are 4 independent parts. A program takes and returns all parts, laid end to end along the dimension named above; an argument that names none is the same for every part.
All inputs are finite; a program needn't handle non-finite values.
Results may differ from a plain program's by a relative error of at most 0.00133.
Values are sent between devices in bfloat16 or wider.
A program may use at most 768 MiB of HBM per device.

v0:
```python
import jax
import jax.numpy as jnp
from jax import lax
from jax.sharding import PartitionSpec as P


def plan_slots(flat_ids, num_experts, capacity):
    num_pairs = flat_ids.shape[0]
    sort_order = jnp.argsort(flat_ids, stable=True)
    sorted_ids = flat_ids[sort_order]
    counts = jnp.bincount(flat_ids, length=num_experts)
    starts = jnp.cumsum(counts) - counts
    pair_rank = jnp.arange(num_pairs) - starts[sorted_ids]
    pair_slot = jnp.zeros_like(sort_order).at[sort_order].set(sorted_ids * capacity + pair_rank)
    slot_src = jnp.minimum(starts[:, None] + jnp.arange(capacity)[None, :], num_pairs - 1)
    return sort_order[slot_src].reshape(-1), pair_slot


def swiglu_experts(tok_buf, w_gate, w_up, w_down):
    gate_h = jnp.einsum('ecd,edf->ecf', tok_buf, w_gate, preferred_element_type=jnp.float32)
    up_h = jnp.einsum('ecd,edf->ecf', tok_buf, w_up, preferred_element_type=jnp.float32)
    hidden = (jax.nn.silu(gate_h) * up_h).astype(jnp.bfloat16)
    return jnp.einsum('ecf,efd->ecd', hidden, w_down, preferred_element_type=jnp.float32).astype(jnp.bfloat16)


def solution(mesh):
    group_size = mesh.shape['ep']

    def device_fn(act_in, router_w, expert_ids, w_gate, w_up, w_down):
        tokens, model_dim = act_in.shape
        top_k = expert_ids.shape[1]
        local_experts = w_gate.shape[0]
        num_experts = local_experts * group_size
        micro_len = tokens // 2
        mean_load = micro_len * top_k // num_experts
        capacity = mean_load + mean_load // 2
        logits = jnp.dot(act_in, router_w, preferred_element_type=jnp.float32)
        gate_vals = jax.nn.softmax(jnp.take_along_axis(logits, expert_ids, axis=1), axis=-1)
        results = []
        for micro_idx in range(2):
            row_start = micro_idx * micro_len
            tok_rows = act_in[row_start:row_start + micro_len]
            slot_pair, pair_slot = plan_slots(expert_ids[row_start:row_start + micro_len].reshape(-1), num_experts, capacity)
            send_buf = tok_rows[slot_pair // top_k].reshape(group_size, local_experts, capacity, model_dim)
            recv_buf = lax.all_to_all(send_buf, 'ep', 0, 2, tiled=True)[0]
            expert_out = swiglu_experts(recv_buf, w_gate, w_up, w_down)
            ret_buf = lax.all_to_all(expert_out[None], 'ep', 2, 0, tiled=True)
            pair_out = ret_buf.reshape(num_experts * capacity, model_dim)[pair_slot]
            pair_out = pair_out.reshape(micro_len, top_k, model_dim).astype(jnp.float32)
            mixed_out = jnp.sum(gate_vals[row_start:row_start + micro_len, :, None] * pair_out, axis=1)
            results.append(mixed_out.astype(jnp.bfloat16))
        return jnp.concatenate(results, axis=0)

    row_spec = P(('dp', 'ep'), None)
    expert_spec = P('ep', None, None)
    return jax.shard_map(device_fn, mesh=mesh,
                         in_specs=(row_spec, P(None, None), row_spec, expert_spec, expert_spec, expert_spec),
                         out_specs=row_spec, check_vma=False)
```

profile of v0, /device:TPU:21, one launch (start us, length us, event | category | flops | bytes accessed | tf_op | source)
XLA Modules:
  0.0 424.2 jit_solution(4598655020982721974)
XLA Ops:
  9.7 5.0 %gather_fusion = s32[768]{0:T(1024)S(1)} fusion(s32[512]{0:T(512)S(1)} %get-tuple-element.7, s32[1024]{0:T(1024)S(1)} %pad_clamp_fusion.7), kind=kCustom, calls=%fused_computation | custom fusion | bytes 9216 | tf_op jit(solution)/shard_map/gather | solution.py:16
  14.8 4.3 %gather_fusion.1 = bf16[768,2048]{1,0:T(8,128)(2,1)} fusion(bf16[64,2048]{1,0:T(8,128)(2,1)S(1)} %get-tuple-element.127, s32[1024]{0:T(1024)S(1)} %pad_clamp_fusion.6), kind=kCustom, calls=%fused_computation.1 | custom fusion | bytes 6294528 | tf_op jit(solution)/shard_map/gather | solution.py:44
  19.1 6.1 %reshape.398 = bf16[16,4,12,2048]{3,2,1,0:T(8,128)(2,1)} reshape(bf16[768,2048]{1,0:T(8,128)(2,1)} %gather_fusion.1) | data formatting | bytes 6291456 | tf_op jit(solution)/shard_map/reshape | solution.py:44
  25.2 6.6 %copy.61 = bf16[16,4,12,2048]{3,1,2,0:T(4,128)(2,1)} copy(bf16[16,4,12,2048]{3,2,1,0:T(8,128)(2,1)} %reshape.398) | data formatting | bytes 6291456 | tf_op jit(solution)/shard_map/reshape | solution.py:44
  31.8 10.7 %all-to-all-start = ((bf16[16,4,12,2048]{3,1,2,0:T(4,128)(2,1)}), bf16[16,4,12,2048]{3,1,2,0:T(4,128)(2,1)}, u32[]{:S(2)}, u32[]{:S(2)}) async-start(bf16[16,4,12,2048]{3,1,2,0:T(4,128)(2,1)} %copy.61), calls=%async_computation | async-start | bytes 6291456 | tf_op jit(solution)/shard_map/all_to_all | solution.py:45
  42.7 4.3 %scatter_custom_fusion.2 = s32[64]{0:T(128)S(1)} fusion(s32[512]{0:T(512)S(1)} %reshape.638, s32[512]{0:T(512)S(1)} %broadcast.591, s32[]{:T(128)} %constant.55.clone.1), kind=kCustom, calls=%fused_computation.204 | custom fusion | flops 512 | bytes 260 | tf_op jit(solution)/shard_map/scatter-add | solution.py:11
  51.6 5.0 %gather_fusion.4 = s32[768]{0:T(1024)S(1)} fusion(s32[512]{0:T(512)S(1)} %get-tuple-element.8, s32[1024]{0:T(1024)S(1)} %pad_clamp_fusion.3), kind=kCustom, calls=%fused_computation.4 | custom fusion | bytes 9216 | tf_op jit(solution)/shard_map/gather | solution.py:16
  56.7 4.3 %gather_fusion.5 = bf16[768,2048]{1,0:T(8,128)(2,1)} fusion(bf16[64,2048]{1,0:T(8,128)(2,1)S(1)} %get-tuple-element.128, s32[1024]{0:T(1024)S(1)} %pad_clamp_fusion.2), kind=kCustom, calls=%fused_computation.5 | custom fusion | bytes 6294528 | tf_op jit(solution)/shard_map/gather | solution.py:44
  61.1 6.1 %reshape.404 = bf16[16,4,12,2048]{3,2,1,0:T(8,128)(2,1)} reshape(bf16[768,2048]{1,0:T(8,128)(2,1)} %gather_fusion.5) | data formatting | bytes 6291456 | tf_op jit(solution)/shard_map/reshape | solution.py:44
  67.1 6.6 %copy.70 = bf16[16,4,12,2048]{3,1,2,0:T(4,128)(2,1)} copy(bf16[16,4,12,2048]{3,2,1,0:T(8,128)(2,1)} %reshape.404) | data formatting | bytes 6291456 | tf_op jit(solution)/shard_map/reshape | solution.py:44
  73.7 39.5 %all-to-all-done = bf16[16,4,12,2048]{3,1,2,0:T(4,128)(2,1)} async-done(((bf16[16,4,12,2048]{3,1,2,0:T(4,128)(2,1)}), bf16[16,4,12,2048]{3,1,2,0:T(4,128)(2,1)}, u32[]{:S(2)}, u32[]{:S(2)}) %all-to-all-start) | async-done | bytes 3145760 | tf_op jit(solution)/shard_map/all_to_all | solution.py:45
  113.3 7.5 %all-to-all-start.2 = ((bf16[16,4,12,2048]{3,1,2,0:T(4,128)(2,1)}), bf16[16,4,12,2048]{3,1,2,0:T(4,128)(2,1)S(1)}, u32[]{:S(2)}, u32[]{:S(2)}) async-start(bf16[16,4,12,2048]{3,1,2,0:T(4,128)(2,1)} %copy.70), calls=%async_computation.2 | async-start | bytes 6291456 | tf_op jit(solution)/shard_map/all_to_all | solution.py:45
  120.8 14.4 %fusion.8 = f32[4,192,1024]{2,1,0:T(8,128)} fusion(bf16[4,2048,1024]{2,1,0:T(8,128)(2,1)} %param.10, bf16[4,192,2048]{2,0,1:T(4,128)(2,1)} %bitcast.4), kind=kOutput, calls=%fused_computation.27 | convolution fusion | flops 3221225472 | bytes 23068672 | tf_op jit(solution)/shard_map/ecd,edf->ecf/dot_general | solution.py:21
  135.2 19.0 %fusion.2 = bf16[1,4,192,2048]{3,2,1,0:T(8,128)(2,1)} fusion(bf16[4,1024,2048]{2,1,0:T(8,128)(2,1)} %param.11, f32[4,192,1024]{2,1,0:T(8,128)} %fusion.8, bf16[4,2048,1024]{2,1,0:T(8,128)(2,1)} %param.9, bf16[4,192,2048]{2,0,1:T(4,128)(2,1)} %bitcast.4), kind=kOutput, calls=%fused_computation.21 | convolution fusion | flops 6448742400 | bytes 42991616 | tf_op jit(solution)/shard_map/ecf,efd->ecd/dot_general | solution.py:23
  154.2 6.0 %copy.64 = bf16[1,4,192,2048]{3,1,0,2:T(4,128)(2,1)} copy(bf16[1,4,192,2048]{3,2,1,0:T(8,128)(2,1)} %fusion.2) | data formatting | bytes 6291456 | tf_op jit(solution)/shard_map/broadcast_in_dim | solution.py:47
  160.2 31.1 %all-to-all-done.2 = bf16[16,4,12,2048]{3,1,2,0:T(4,128)(2,1)S(1)} async-done(((bf16[16,4,12,2048]{3,1,2,0:T(4,128)(2,1)}), bf16[16,4,12,2048]{3,1,2,0:T(4,128)(2,1)S(1)}, u32[]{:S(2)}, u32[]{:S(2)}) %all-to-all-start.2) | async-done | bytes 3145760 | tf_op jit(solution)/shard_map/all_to_all | solution.py:45
  192.9 6.7 %all-to-all-start.1 = ((bf16[1,4,192,2048]{3,1,0,2:T(4,128)(2,1)}), bf16[1,4,192,2048]{3,1,0,2:T(4,128)(2,1)S(1)}, u32[]{:S(2)}, u32[]{:S(2)}) async-start(bf16[1,4,192,2048]{3,1,0,2:T(4,128)(2,1)} %copy.64), calls=%async_computation.1 | async-start | bytes 6291456 | tf_op jit(solution)/shard_map/all_to_all | solution.py:47
  199.6 14.5 %fusion.4 = f32[4,192,1024]{2,1,0:T(8,128)} fusion(bf16[4,2048,1024]{2,1,0:T(8,128)(2,1)} %param.10, bf16[4,192,2048]{2,0,1:T(4,128)(2,1)} %bitcast.181), kind=kOutput, calls=%fused_computation.23 | convolution fusion | flops 3221225472 | bytes 23068672 | tf_op jit(solution)/shard_map/ecd,edf->ecf/dot_general | solution.py:21
  214.1 19.0 %fusion.3 = bf16[1,4,192,2048]{3,2,1,0:T(8,128)(2,1)} fusion(bf16[4,1024,2048]{2,1,0:T(8,128)(2,1)} %param.11, f32[4,192,1024]{2,1,0:T(8,128)} %fusion.4, bf16[4,2048,1024]{2,1,0:T(8,128)(2,1)} %param.9, bf16[4,192,2048]{2,0,1:T(4,128)(2,1)} %bitcast.182), kind=kOutput, calls=%fused_computation.22 | convolution fusion | flops 6448742400 | bytes 42991616 | tf_op jit(solution)/shard_map/ecf,efd->ecd/dot_general | solution.py:23
  233.2 6.0 %copy.73 = bf16[1,4,192,2048]{3,1,0,2:T(4,128)(2,1)} copy(bf16[1,4,192,2048]{3,2,1,0:T(8,128)(2,1)} %fusion.3) | data formatting | bytes 6291456 | tf_op jit(solution)/shard_map/broadcast_in_dim | solution.py:47
  239.2 31.2 %all-to-all-done.1 = bf16[1,4,192,2048]{3,1,0,2:T(4,128)(2,1)S(1)} async-done(((bf16[1,4,192,2048]{3,1,0,2:T(4,128)(2,1)}), bf16[1,4,192,2048]{3,1,0,2:T(4,128)(2,1)S(1)}, u32[]{:S(2)}, u32[]{:S(2)}) %all-to-all-start.1) | async-done | bytes 3145760 | tf_op jit(solution)/shard_map/all_to_all | solution.py:47
  270.4 6.7 %all-to-all-start.3 = ((bf16[1,4,192,2048]{3,1,0,2:T(4,128)(2,1)}), bf16[1,4,192,2048]{3,1,0,2:T(4,128)(2,1)}, u32[]{:S(2)}, u32[]{:S(2)}) async-start(bf16[1,4,192,2048]{3,1,0,2:T(4,128)(2,1)} %copy.73), calls=%async_computation.3 | async-start | bytes 6291456 | tf_op jit(solution)/shard_map/all_to_all | solution.py:47
  283.6 4.5 %compare_select_fusion.13 = (s32[512,1]{0,1:T(1,128)S(1)}, s32[512,1]{0,1:T(1,128)S(1)}) fusion(s32[]{:T(128)} %bitcast.68, s32[]{:T(128)} %bitcast.69, s32[]{:T(128)} %bitcast.70, s32[]{:T(128)} %bitcast.71, s32[]{:T(128)} %bitcast.72, s32[]{:T(128)} %bitcast.74, s32[]{:T(128)} %bitcast.73, s32[512,1]{0,1:T(1,128)S(1)} %bitcast.183), kind=kLoop, calls=%fused_computation.163 | loop fusion | flops 7680 | bytes 6172 | tf_op jit(solution)/shard_map/gather | solution.py:13
  288.4 35.3 %fusion.27 = s32[512]{0:T(512)S(1)} fusion(pred[512]{0:T(512)(128)(4,1)S(1)} %get-tuple-element.65, pred[512]{0:T(512)(128)(4,1)S(1)} %get-tuple-element.64, pred[512]{0:T(512)(128)(4,1)S(1)} %get-tuple-element.63, pred[512]{0:T(512)(128)(4,1)S(1)} %get-tuple-element.62, pred[512]{0:T(512)(128)(4,1)S(1)} %get-tuple-element.61, ...), kind=kLoop, calls=%fused_computation.197 | loop fusion | flops 30720 | bytes 35556 | tf_op jit(solution)/shard_map/add | solution.py:14
  337.2 35.7 %fusion.26 = s32[512]{0:T(512)S(1)} fusion(pred[512]{0:T(512)(128)(4,1)S(1)} %get-tuple-element.122, pred[512]{0:T(512)(128)(4,1)S(1)} %get-tuple-element.121, pred[512]{0:T(512)(128)(4,1)S(1)} %get-tuple-element.120, pred[512]{0:T(512)(128)(4,1)S(1)} %get-tuple-element.119, pred[512]{0:T(512)(128)(4,1)S(1)} %get-tuple-element.118, ...), kind=kLoop, calls=%fused_computation.195 | loop fusion | flops 30720 | bytes 35556 | tf_op jit(solution)/shard_map/add | solution.py:14
  376.9 7.3 %gather_fusion.8 = f32[1024]{0:T(1024)S(1)} fusion(f32[128,64]{0,1:T(8,128)S(1)} %fusion.49, s32[1024]{0:T(1024)S(1)} %reshape.614), kind=kCustom, calls=%fused_computation.8 | custom fusion | bytes 16384 | tf_op jit(solution)/shard_map/jit(take_along_axis)/gather | solution.py:38
  384.7 4.2 %copy.65 = bf16[16,1,4,12,2048]{4,3,2,0,1:T(8,128)(2,1)} copy(bf16[16,1,4,12,2048]{4,2,3,0,1:T(4,128)(2,1)S(1)} %bitcast.180) | data formatting | bytes 6291456 | tf_op jit(solution)/shard_map/all_to_all | solution.py:47
  388.9 4.7 %reshape.399 = bf16[768,2048]{1,0:T(8,128)(2,1)S(1)} reshape(bf16[16,1,4,12,2048]{4,3,2,0,1:T(8,128)(2,1)} %copy.65) | data formatting | bytes 6291456 | tf_op jit(solution)/shard_map/reshape | solution.py:48
  393.7 6.1 %copy.74 = bf16[16,1,4,12,2048]{4,3,2,0,1:T(8,128)(2,1)} copy(bf16[16,1,4,12,2048]{4,2,3,0,1:T(4,128)(2,1)} %bitcast.85) | data formatting | bytes 6291456 | tf_op jit(solution)/shard_map/all_to_all | solution.py:47
  399.8 6.2 %reshape.405 = bf16[768,2048]{1,0:T(8,128)(2,1)} reshape(bf16[16,1,4,12,2048]{4,3,2,0,1:T(8,128)(2,1)} %copy.74) | data formatting | bytes 6291456 | tf_op jit(solution)/shard_map/reshape | solution.py:48
  409.3 8.2 %gather_fusion.7 = bf16[512,2048]{1,0:T(8,128)(2,1)} fusion(bf16[768,2048]{1,0:T(8,128)(2,1)} %reshape.405, s32[1024]{0:T(1024)S(1)} %pad_clamp_fusion), kind=kCustom, calls=%fused_computation.7 | custom fusion | bytes 4196352 | tf_op jit(solution)/shard_map/gather | solution.py:48
  417.4 5.8 %fusion = (bf16[64,2048]{1,0:T(8,128)(2,1)S(1)}, bf16[64,2048]{1,0:T(8,128)(2,1)S(1)}) fusion(bf16[512,2048]{1,0:T(8,128)(2,1)} %gather_fusion.7, f32[64,8]{1,0:T(8,128)S(1)} %copy.66, bf16[512,2048]{1,0:T(8,128)(2,1)S(1)} %copy-done.10, f32[64,8]{1,0:T(8,128)S(1)} %copy.57), kind=kLoop, calls=%fused_computation.14 | loop fusion | flops 6029312 | bytes 4722688 | tf_op jit(solution)/shard_map/reduce_sum | solution.py:50
  (106 shorter events, 44.9 us)
Async XLA Ops:
  0.0 375.5 %copy-start = (bf16[2048,64]{0,1:T(8,128)(2,1)S(1)}, bf16[2048,64]{0,1:T(8,128)(2,1)}, u32[]{:S(2)}) copy-start(bf16[2048,64]{0,1:T(8,128)(2,1)} %param.7) | copy-start | bytes 786436
  5.4 0.5 copy-start.13
  5.6 9.1 %copy-start.7 = (s32[512]{0:T(512)}, s32[512]{0:T(512)S(1)}, u32[]{:S(2)}) copy-start(s32[512]{0:T(512)S(1)} %reshape.394) | copy-start | bytes 6148
  9.7 5.0 %copy-start.3 = (s32[512]{0:T(512)}, s32[512]{0:T(512)S(1)}, u32[]{:S(2)}) copy-start(s32[512]{0:T(512)S(1)} %get-tuple-element.7) | copy-start | bytes 6148
  9.7 5.1 %copy-start.15 = (bf16[128,2048]{1,0:T(8,128)(2,1)S(1)}, bf16[128,2048]{1,0:T(8,128)(2,1)}, u32[]{:S(2)}) copy-start(bf16[128,2048]{1,0:T(8,128)(2,1)} %param.6) | copy-start | bytes 1572868
  31.8 81.5 %all-to-all-start = ((bf16[16,4,12,2048]{3,1,2,0:T(4,128)(2,1)}), bf16[16,4,12,2048]{3,1,2,0:T(4,128)(2,1)}, u32[]{:S(2)}, u32[]{:S(2)}) async-start(bf16[16,4,12,2048]{3,1,2,0:T(4,128)(2,1)} %copy.61), calls=%async_computation | async-start | bytes 6291456 | tf_op jit(solution)/shard_map/all_to_all | solution.py:45
  47.3 0.5 copy-start.11
  47.5 9.1 %copy-start.5 = (s32[512]{0:T(512)}, s32[512]{0:T(512)S(1)}, u32[]{:S(2)}) copy-start(s32[512]{0:T(512)S(1)} %reshape.400) | copy-start | bytes 6148
  51.6 5.0 %copy-start.1 = (s32[512]{0:T(512)}, s32[512]{0:T(512)S(1)}, u32[]{:S(2)}) copy-start(s32[512]{0:T(512)S(1)} %get-tuple-element.8) | copy-start | bytes 6148
  113.3 77.9 %all-to-all-start.2 = ((bf16[16,4,12,2048]{3,1,2,0:T(4,128)(2,1)}), bf16[16,4,12,2048]{3,1,2,0:T(4,128)(2,1)S(1)}, u32[]{:S(2)}, u32[]{:S(2)}) async-start(bf16[16,4,12,2048]{3,1,2,0:T(4,128)(2,1)} %copy.70), calls=%async_computation.2 | async-start | bytes 6291456 | tf_op jit(solution)/shard_map/all_to_all | solution.py:45
  191.2 1.7 copy-start.9
  192.9 77.5 %all-to-all-start.1 = ((bf16[1,4,192,2048]{3,1,0,2:T(4,128)(2,1)}), bf16[1,4,192,2048]{3,1,0,2:T(4,128)(2,1)S(1)}, u32[]{:S(2)}, u32[]{:S(2)}) async-start(bf16[1,4,192,2048]{3,1,0,2:T(4,128)(2,1)} %copy.64), calls=%async_computation.1 | async-start | bytes 6291456 | tf_op jit(solution)/shard_map/all_to_all | solution.py:47
  239.2 38.0 %copy-start.4 = (s32[512]{0:T(512)S(1)}, s32[512]{0:T(512)}, u32[]{:S(2)}) copy-start(s32[512]{0:T(512)} %copy-done.3) | copy-start | bytes 6148
  239.2 38.0 %copy-start.8 = (s32[512]{0:T(512)S(1)}, s32[512]{0:T(512)}, u32[]{:S(2)}) copy-start(s32[512]{0:T(512)} %copy-done.7) | copy-start | bytes 6148
  239.2 41.5 %copy-start.14 = (s32[64]{0:T(128)S(1)}, s32[64]{0:T(128)}, u32[]{:S(2)}) copy-start(s32[64]{0:T(128)} %copy-done.13) | copy-start | bytes 772
  239.2 87.0 %copy-start.2 = (s32[512]{0:T(512)S(1)}, s32[512]{0:T(512)}, u32[]{:S(2)}) copy-start(s32[512]{0:T(512)} %copy-done.1) | copy-start | bytes 6148
  239.2 87.0 %copy-start.6 = (s32[512]{0:T(512)S(1)}, s32[512]{0:T(512)}, u32[]{:S(2)}) copy-start(s32[512]{0:T(512)} %copy-done.5) | copy-start | bytes 6148
  270.4 123.2 %all-to-all-start.3 = ((bf16[1,4,192,2048]{3,1,0,2:T(4,128)(2,1)}), bf16[1,4,192,2048]{3,1,0,2:T(4,128)(2,1)}, u32[]{:S(2)}, u32[]{:S(2)}) async-start(bf16[1,4,192,2048]{3,1,0,2:T(4,128)(2,1)} %copy.73), calls=%async_computation.3 | async-start | bytes 6291456 | tf_op jit(solution)/shard_map/all_to_all | solution.py:47
  277.1 52.6 %copy-start.12 = (s32[64]{0:T(128)S(1)}, s32[64]{0:T(128)}, u32[]{:S(2)}) copy-start(s32[64]{0:T(128)} %copy-done.11) | copy-start | bytes 772
  277.1 98.2 %copy-start.16 = (s32[128,8]{0,1:T(8,128)S(1)}, s32[128,8]{0,1:T(8,128)}, u32[]{:S(2)}) copy-start(s32[128,8]{0,1:T(8,128)} %param.8) | copy-start | bytes 12292
  409.3 8.2 %copy-start.10 = (bf16[512,2048]{1,0:T(8,128)(2,1)S(1)}, bf16[512,2048]{1,0:T(8,128)(2,1)}, u32[]{:S(2)}) copy-start(bf16[512,2048]{1,0:T(8,128)(2,1)} %gather_fusion.3) | copy-start | bytes 6291460
where the time goes:
time: 432 us; the launch traced here: 424 us
  local copies, waits for them, and re-layouts  117 us (27%)
  other arithmetic  105 us (24%)
  waiting for transfers between devices  102 us (24%)
  matrix products  68.3 us (16%)
  starting transfers between devices  31.6 us (7%)
    add x2, other arithmetic, plan_slots(): sorted_ids * capacity + pair_rank  71 us
    all_to_all x2, waiting for transfers between devices, device_fn(): recv_buf = lax.all_to_all(send_buf, 'ep', 0, 2, tiled=True)[0]  70.6 us
    dot_general x2, matrix products, swiglu_experts(): jnp.einsum('ecf,efd->ecd', hidden, w_down, preferred_element_type=jnp.flo...  38 us
    all_to_all x2, waiting for transfers between devices, device_fn(): ret_buf = lax.all_to_all(expert_out[None], 'ep', 2, 0, tiled=True)  31.3 us
    dot_general x2, matrix products, swiglu_experts(): jnp.einsum('ecd,edf->ecf', tok_buf, w_up, preferred_element_type=jnp.floa...  28.9 us
    reshape x4, local copies, waits for them, and re-layouts, device_fn(): tok_rows[slot_pair // top_k]  25.4 us
    all_to_all x2, starting transfers between devices, device_fn(): recv_buf = lax.all_to_all(send_buf, 'ep', 0, 2, tiled=True)[0]  18.2 us
    all_to_all x2, starting transfers between devices, device_fn(): ret_buf = lax.all_to_all(expert_out[None], 'ep', 2, 0, tiled=True)  13.4 us
  transfers between devices with their start and end apart: 4, of which 3 were waited for; matrix products, arithmetic and copies ran while one was open for 53% of the time, Pallas kernels for 0%

commit v1 on v0

v1 whole, which is shorter than its diff:
```python
import functools

import jax
import jax.numpy as jnp
from jax import lax
from jax.experimental import pallas as pl
from jax.experimental.pallas import tpu as pltpu
from jax.sharding import PartitionSpec as P

MESH = pl.DeviceIdType.MESH
F32 = jnp.float32
BF16 = jnp.bfloat16

POS = {4: 0, -4: 0, 0: 1, -3: 2, 3: 3, -2: 4, 2: 5, -1: 6, 1: 7}
SIGN = (1, -1)
BACK = ((4, 0), (3, 1), (3, 0), (2, 1), (2, 0), (1, 1), (1, 0))
GU_TILE = 256
DN_TILE = 1024


def dot(a, b):
    return jnp.dot(a, b, preferred_element_type=F32)


def layer_kernel(group, ids_hbm, rw_hbm, x_hbm, wg_hbm, wu_hbm, wd_hbm, out_hbm,
                 xg, meta, ids_v, rw_v, tp, xe, hid, eo, cm, part, sib, inb, outv, wgu, wdn,
                 ag_s, ag_r, dx_s, dx_r, mt_s, mt_r, dm_s, dm_r, rs_s, rs_r, sb_s, sb_r,
                 gu_sem, dn_sem, ld_sem, st_sem):
    micro = 64
    half = 32
    me = lax.axis_index('ep')
    core = lax.rem(me, 2)
    other = 1 - core
    nbr = (lax.rem(me + 2, group), lax.rem(me + group - 2, group))
    sibling = me + 1 - 2 * core
    local_experts = wg_hbm.shape[0]
    slots = xe.shape[1] // 4

    def remote(src, dst, ssem, rsem, dev):
        return pltpu.make_async_remote_copy(src_ref=src, dst_ref=dst, send_sem=ssem, recv_sem=rsem,
                                            device_id={'ep': dev}, device_id_type=MESH)

    def gu_copies(e, f):
        cols = pl.ds(f * GU_TILE, GU_TILE)
        return (pltpu.make_async_copy(wg_hbm.at[e, :, cols], wgu.at[f, 0], gu_sem.at[f, 0]),
                pltpu.make_async_copy(wu_hbm.at[e, :, cols], wgu.at[f, 1], gu_sem.at[f, 1]))

    def dn_copy(e, n):
        return pltpu.make_async_copy(wd_hbm.at[e, :, pl.ds(n * DN_TILE, DN_TILE)], wdn.at[n], dn_sem.at[n])

    def x_rows(m, pos, c, start, size):
        row = pl.multiple_of((pos % 2) * 2 * micro + c * micro + start, half)
        return xg.at[m, pos // 2, pl.ds(row, size)]

    def ag_copy(m, d, k, piece):
        src = x_rows(m, POS[-SIGN[d] * k], core, piece * half, half)
        dst = x_rows(m, POS[-SIGN[d] * (k + 1)], core, piece * half, half)
        return remote(src, dst, ag_s.at[m, d, k, piece], ag_r.at[m, d, k, piece], nbr[d])

    def ag_has(d, k, piece):
        return k < 3 or piece == d

    def dx_copy(m, pos, c):
        ref = x_rows(m, pos, c, 0, micro)
        return remote(ref, ref, dx_s.at[m, pos], dx_r.at[m, pos], sibling)

    def mt_copy(d, k):
        return remote(meta.at[POS[-SIGN[d] * k], core], meta.at[POS[-SIGN[d] * (k + 1)], core],
                      mt_s.at[d, k], mt_r.at[d, k], nbr[d])

    def mt_has(d, k):
        return k < 3 or d == 0

    def dm_copy(pos, c):
        return remote(meta.at[pos, c], meta.at[pos, c], dm_s.at[pos], dm_r.at[pos], sibling)

    def send_own(m):
        for piece in range(2):
            for d in range(2):
                ag_copy(m, d, 0, piece).start()
        dx_copy(m, POS[0], core).start()

    def ag_event(m, k, piece):
        for d in range(2):
            if ag_has(d, k, piece):
                ag_copy(m, d, k, piece).wait_recv()
                if k < 3 and ag_has(d, k + 1, piece):
                    ag_copy(m, d, k + 1, piece).start()
        if piece == 1:
            for pos in ((POS[4],) if k == 3 else (POS[-(k + 1)], POS[k + 1])):
                dx_copy(m, pos, core).start()

    def mt_event(k):
        for d in range(2):
            if mt_has(d, k):
                mt_copy(d, k).wait_recv()
                if k < 3 and mt_has(d, k + 1):
                    mt_copy(d, k + 1).start()
                dm_copy(POS[-SIGN[d] * (k + 1)], core).start()

    def make_meta():
        for m in range(2):
            rows = x_rows(m, POS[0], core, 0, micro)
            tp[0, m * micro:(m + 1) * micro, 0:rw_v.shape[1]] = dot(rows[...], rw_v[...])
        tp[1, :, 0:8] = ids_v[...].astype(F32)
        logits = tp[0].T
        ids = tp[1].T[0:8]
        expert = lax.broadcasted_iota(jnp.int32, (rw_v.shape[1], 2 * micro), 0).astype(F32)
        logits = logits[0:rw_v.shape[1]]
        picked = []
        for j in range(8):
            picked.append(jnp.sum(jnp.where(expert == ids[j:j + 1], logits, 0.0), axis=0, keepdims=True))
        picked = jnp.concatenate(picked, axis=0)
        top = jnp.exp(picked - jnp.max(picked, axis=0, keepdims=True))
        gates = top / jnp.sum(top, axis=0, keepdims=True)
        both = jnp.concatenate([ids, gates], axis=0)
        turned = pltpu.roll(both, micro, 1)
        mine = lax.broadcasted_iota(jnp.int32, both.shape, 1) // micro == core
        for m in range(2):
            meta[POS[0], core, m] = jnp.where(mine, jnp.where(core == m, both, turned), 0.0)

    def gather(m, p):
        token = 4 * micro
        info = jnp.concatenate([meta[2 * p, 0, m] + meta[2 * p, 1, m],
                                meta[2 * p + 1, 0, m] + meta[2 * p + 1, 1, m]], axis=1)
        ids, gates = info[0:8], info[8:16]
        chosen, weight = [], []
        for e in range(local_experts):
            hit = ids == (me * local_experts + e).astype(F32)
            chosen.append(jnp.sum(jnp.where(hit, 1.0, 0.0), axis=0, keepdims=True))
            weight.append(jnp.sum(jnp.where(hit, gates, 0.0), axis=0, keepdims=True))
        stacked = jnp.concatenate(chosen + [jnp.zeros((16 - local_experts, token), F32)], axis=0)
        row = lax.broadcasted_iota(jnp.int32, (token, token), 0)
        col = lax.broadcasted_iota(jnp.int32, (token, token), 1)
        before = jnp.where(row < col, 1.0, 0.0).astype(BF16)
        eye = jnp.where(row == col, 1.0, 0.0).astype(BF16)
        rank = dot(stacked.astype(BF16), before)
        slot = lax.broadcasted_iota(jnp.int32, (slots, token), 0).astype(F32)
        pick, mix = [], []
        for e in range(local_experts):
            place = jnp.where(chosen[e] > 0.5, rank[e:e + 1], -1.0)
            at = slot == place
            pick.append(jnp.where(at, 1.0, 0.0))
            mix.append(jnp.where(at, weight[e], 0.0))
        pick = jnp.concatenate(pick, axis=0).astype(BF16)
        rest = jnp.concatenate(mix, axis=0)
        for i in range(3):
            term = rest.astype(BF16)
            rest = rest - term.astype(F32)
            turned = lax.dot_general(eye, term, (((1,), (1,)), ((), ())), preferred_element_type=F32)
            cm[p, i] = turned.astype(BF16)
        for n in range(0, xg.shape[-1], 512):
            rows = dot(pick, xg[m, p, :, n:n + 512]).astype(BF16)
            for e in range(local_experts):
                xe[e, pl.ds(pl.multiple_of(p * slots, 16), slots), n:n + 512] = rows[e * slots:(e + 1) * slots]

    def expert(e, more):
        nxt = lax.rem(e + 1, local_experts)
        for f in range(4):
            for cp in gu_copies(e, f):
                cp.wait()
            a = dot(xe[e], wgu[f, 0])
            b = dot(xe[e], wgu[f, 1])
            hid[:, f * GU_TILE:(f + 1) * GU_TILE] = (a * jax.nn.sigmoid(a) * b).astype(BF16)

            @pl.when(more)
            def _():
                for cp in gu_copies(nxt, f):
                    cp.start()
        for n in range(2):
            dn_copy(e, n).wait()
            for s in range(0, DN_TILE, 512):
                o = dot(hid[...], wdn[n, :, s:s + 512]).astype(BF16)
                for p in range(4):
                    eo[p, pl.ds(pl.multiple_of(e * slots, 16), slots),
                       n * DN_TILE + s:n * DN_TILE + s + 512] = o[p * slots:(p + 1) * slots]

            @pl.when(more)
            def _():
                dn_copy(nxt, n).start()

    def combine(pos):
        p, top = pos // 2, (pos % 2) * 2 * micro

        @pl.loop(0, xg.shape[-1] // 512)
        def _(i):
            cols = pl.ds(pl.multiple_of(i * 512, 512), 512)
            o = eo[p, :, cols]
            acc = dot(cm[p, 0, top:top + 2 * micro], o)
            acc = acc + dot(cm[p, 1, top:top + 2 * micro], o)
            acc = acc + dot(cm[p, 2, top:top + 2 * micro], o)
            part[pos, 0, :, cols] = acc[:micro]
            part[pos, 1, :, cols] = acc[micro:]

    def sb_copy(m, pos):
        return remote(part.at[pos, other], sib.at[m, pos], sb_s.at[m, pos], sb_r.at[m, pos], sibling)

    def back_item(d, j):
        dist, rows = BACK[j]
        return POS[SIGN[d] * dist], (rows if d == 0 else 1 - rows)

    def rs_copy(m, d, j):
        pos, r = back_item(d, j)
        return remote(part.at[pos, core, pl.ds(r * half, half)], inb.at[m, d, j],
                      rs_s.at[m, d, j], rs_r.at[m, d, j], nbr[d])

    here = set()

    def need_sib(m, pos):
        if (m, pos) not in here:
            here.add((m, pos))
            sb_copy(m, pos).wait_recv()

    def back(m, j):
        for d in range(2):
            pos, r = back_item(d, j)
            need_sib(m, pos)
            rows = pl.ds(r * half, half)
            acc = part[pos, core, rows] + sib[m, pos, rows]
            if j >= 2:
                rs_copy(m, d, j - 2).wait_recv()
                acc = acc + inb[m, d, j - 2]
            part[pos, core, rows] = acc
            rs_copy(m, d, j).start()

    def st_copy(m, r):
        rows = pl.ds(m * micro + r * half, half)
        return pltpu.make_async_copy(outv.at[rows], out_hbm.at[rows], st_sem.at[m, r])

    def finish(m, r):
        pos = POS[0]
        need_sib(m, pos)
        rows = pl.ds(r * half, half)
        acc = part[pos, core, rows] + sib[m, pos, rows]
        for d in range(2):
            j = 5 if (r == 1) == (d == 0) else 6
            if (m, d, j) not in here:
                here.add((m, d, j))
                rs_copy(m, d, j).wait_recv()
            acc = acc + inb[m, d, j]
        outv[pl.ds(m * micro + r * half, half)] = acc.astype(BF16)
        st_copy(m, r).start()

    def combine_send(m, pos):
        combine(pos)
        sb_copy(m, pos).start()

    def part_free(m, pos):
        sb_copy(m, pos).wait_send()
        for d in range(2):
            for j in range(7):
                if back_item(d, j)[0] == pos:
                    rs_copy(m, d, j).wait_send()

    def pair_wait(m, p):
        for pos in (2 * p, 2 * p + 1):
            dx_copy(m, pos, other).wait_recv()
            if m == 0:
                dm_copy(pos, other).wait_recv()

    loads = [pltpu.make_async_copy(x_hbm.at[pl.ds(m * micro, micro)], x_rows(m, POS[0], core, 0, micro), ld_sem.at[m])
             for m in range(2)]
    loads.append(pltpu.make_async_copy(ids_hbm, ids_v, ld_sem.at[2]))
    loads.append(pltpu.make_async_copy(rw_hbm, rw_v, ld_sem.at[3]))
    for cp in loads:
        cp.start()

    barrier = pltpu.get_barrier_semaphore()
    for dev in (nbr[0], nbr[1], sibling):
        pl.semaphore_signal(barrier, inc=1, device_id={'ep': dev}, device_id_type=MESH)
    for f in range(4):
        for cp in gu_copies(0, f):
            cp.start()
    for n in range(2):
        dn_copy(0, n).start()
    loads[0].wait()
    pl.semaphore_wait(barrier, 3)

    send_own(0)
    for cp in loads[1:]:
        cp.wait()
    make_meta()
    for d in range(2):
        mt_copy(d, 0).start()
    dm_copy(POS[0], core).start()

    ag_event(0, 0, 0)
    ag_event(0, 0, 1)
    mt_event(0)
    ag_event(0, 1, 0)
    ag_event(0, 1, 1)
    mt_event(1)
    pair_wait(0, 3)
    gather(0, 3)
    ag_event(0, 2, 0)
    ag_event(0, 2, 1)
    mt_event(2)
    send_own(1)
    pair_wait(0, 2)
    gather(0, 2)
    pair_wait(0, 1)
    gather(0, 1)
    ag_event(0, 3, 0)
    ag_event(0, 3, 1)
    mt_event(3)
    pair_wait(0, 0)
    gather(0, 0)

    @pl.loop(0, local_experts)
    def _(e):
        expert(e, e >= 0)
        for i, (k, piece) in enumerate(((0, 0), (0, 1), (1, 0), (1, 1))):
            @pl.when(e == i)
            def _():
                ag_event(1, k, piece)

    combine_send(0, POS[4])
    combine_send(0, POS[-3])
    combine_send(0, POS[3])
    ag_event(1, 2, 0)
    ag_event(1, 2, 1)
    back(0, 0)
    back(0, 1)
    for pos in (4, 5, 6, 7, 1):
        combine_send(0, pos)
    ag_event(1, 3, 0)
    ag_event(1, 3, 1)
    for p in range(4):
        pair_wait(1, p)

    @pl.loop(0, 4)
    def _(p):
        gather(1, p)

    for j in range(2, 7):
        for d in range(2):
            need_sib(0, back_item(d, j)[0])

    @pl.loop(0, local_experts)
    def _(e):
        expert(e, e < local_experts - 1)
        for i, j in ((0, 2), (2, 3), (3, 4)):
            @pl.when(e == i)
            def _():
                back(0, j)

    back(0, 5)
    for pos in (0, 2, 3):
        part_free(0, pos)
        combine_send(1, pos)
    back(0, 6)
    back(1, 0)
    back(1, 1)
    for pos in (4, 5):
        part_free(0, pos)
        combine_send(1, pos)
    finish(0, 0)
    finish(0, 1)
    for pos in (6, 7, 1):
        part_free(0, pos)
        combine_send(1, pos)
    for j in range(2, 7):
        back(1, j)
    finish(1, 0)
    finish(1, 1)

    for m in range(2):
        for d in range(2):
            for k in range(4):
                for piece in range(2):
                    if ag_has(d, k, piece):
                        ag_copy(m, d, k, piece).wait_send()
        for pos in range(8):
            dx_copy(m, pos, core).wait_send()
    for d in range(2):
        for k in range(4):
            if mt_has(d, k):
                mt_copy(d, k).wait_send()
    for pos in range(8):
        dm_copy(pos, core).wait_send()
        part_free(1, pos)
    for m in range(2):
        for r in range(2):
            st_copy(m, r).wait()


def solution(mesh):
    group = mesh.shape['ep']

    def device_fn(act_in, router_w, expert_ids, w_gate, w_up, w_down):
        tokens, dim = act_in.shape
        local_experts, _, ffn = w_gate.shape
        micro = tokens // 2
        half = micro // 2
        mean_load = micro * expert_ids.shape[1] // (local_experts * group)
        cap = mean_load + mean_load // 2
        slots = 4 * cap
        dma = pltpu.SemaphoreType.DMA
        scratch = [
            pltpu.VMEM((2, 4, 4 * micro, dim), BF16),
            pltpu.VMEM((8, 2, 2, 16, 2 * micro), F32),
            pltpu.VMEM(expert_ids.shape, jnp.int32),
            pltpu.VMEM(router_w.shape, BF16),
            pltpu.VMEM((2, tokens, 128), F32),
            pltpu.VMEM((local_experts, 4 * slots, dim), BF16),
            pltpu.VMEM((4 * slots, ffn), BF16),
            pltpu.VMEM((4, local_experts * slots, dim), BF16),
            pltpu.VMEM((4, 3, 4 * micro, local_experts * slots), BF16),
            pltpu.VMEM((8, 2, micro, dim), F32),
            pltpu.VMEM((2, 8, micro, dim), F32),
            pltpu.VMEM((2, 2, 7, half, dim), F32),
            pltpu.VMEM((tokens, dim), BF16),
            pltpu.VMEM((4, 2, dim, GU_TILE), BF16),
            pltpu.VMEM((2, ffn, DN_TILE), BF16),
            dma((2, 2, 4, 2)), dma((2, 2, 4, 2)),
            dma((2, 8)), dma((2, 8)),
            dma((2, 4)), dma((2, 4)),
            dma((8,)), dma((8,)),
            dma((2, 2, 7)), dma((2, 2, 7)),
            dma((2, 8)), dma((2, 8)),
            dma((4, 2)), dma((2,)), dma((4,)), dma((2, 2)),
        ]
        return pl.pallas_call(
            functools.partial(layer_kernel, group),
            out_shape=jax.ShapeDtypeStruct((tokens, dim), BF16),
            in_specs=[pl.BlockSpec(memory_space=pl.ANY)] * 6,
            out_specs=pl.BlockSpec(memory_space=pl.ANY),
            scratch_shapes=scratch,
            compiler_params=pltpu.CompilerParams(collective_id=0, has_side_effects=True,
                                                 vmem_limit_bytes=67043328),
            name='moe_layer',
        )(expert_ids, router_w, act_in, w_gate, w_up, w_down)

    row_spec = P(('dp', 'ep'), None)
    expert_spec = P('ep', None, None)
    return jax.shard_map(device_fn, mesh=mesh,
                         in_specs=(row_spec, P(None, None), row_spec, expert_spec, expert_spec, expert_spec),
                         out_specs=row_spec, check_vma=False)
```

time: 432 us -> 149 us (0.34); the launches traced: 424 us -> 148 us
  Pallas kernels: 0 us -> 143 us
  local copies, waits for them, and re-layouts: 117 us -> 5.24 us
  other arithmetic: 105 us -> 0 us
  waiting for transfers between devices: 102 us -> 0 us
  matrix products: 68.3 us -> 0 us
  starting transfers between devices: 31.6 us -> 0 us
    pallas_call x0 -> x1, Pallas kernels: none -> 143 us  [device_fn(): pl.pallas_call(functools.partial(layer_kernel, group), out_shape=jax.Shap...]
    all_to_all x4 -> x0, waiting for transfers between devices: 102 us -> none  [the longest x2 70.6 us: device_fn(): recv_buf = lax.all_to_all(send_buf, 'ep', 0, 2, tiled=True)[0]]
    add x2 -> x0, other arithmetic: 71 us -> none  [plan_slots(): sorted_ids * capacity + pair_rank]
    dot_general x5 -> x0, matrix products: 68.3 us -> none  [the longest x2 38 us: swiglu_experts(): jnp.einsum('ecf,efd->ecd', hidden, w_down, preferred_element_type=jnp.flo...]
    gather x21 -> x0, local copies, waits for them, and re-layouts: 50.3 us -> none  [the longest x2 11.5 us: device_fn(): pair_out = ret_buf.reshape(num_experts * capacity, model_dim)[pair_slot]]
    reshape x8 -> x0, local copies, waits for them, and re-layouts: 36.4 us -> none  [the longest x4 25.4 us: device_fn(): tok_rows[slot_pair // top_k]]
    all_to_all x4 -> x0, starting transfers between devices: 31.6 us -> none  [the longest x2 18.2 us: device_fn(): recv_buf = lax.all_to_all(send_buf, 'ep', 0, 2, tiled=True)[0]]
    broadcast_in_dim x2 -> x0, local copies, waits for them, and re-layouts: 12 us -> none  [device_fn(): ret_buf = lax.all_to_all(expert_out[None], 'ep', 2, 0, tiled=True)]
  transfers between devices with their start and end apart: 4 -> 0, of which waited for: 3 -> 0; matrix products, arithmetic and copies ran while one was open for 53% -> 0% of each run, Pallas kernels for 0% -> 0%
where the time goes in v1:
time: 149 us; the launch traced here: 148 us
  Pallas kernels  143 us (96%)
  local copies, waits for them, and re-layouts  5.24 us (4%)
    pallas_call x1, Pallas kernels, device_fn(): pl.pallas_call(functools.partial(layer_kernel, group), out_shape=jax.Shap...  143 us
    unnamed x3, local copies, waits for them, and re-layouts  5.24 us

profile of v1, /device:TPU:21, one launch (start us, length us, event | category | flops | bytes accessed | tf_op | source)
XLA Modules:
  0.0 148.3 jit_solution(1612938384143673009)
XLA Ops:
  0.0 1.4 copy.7.ids_hbm
  1.4 2.0 %copy.8.rw_hbm = bf16[2048,64]{1,0:T(8,128)(2,1)} copy(bf16[2048,64]{0,1:T(8,128)(2,1)} %param.7) | data formatting | bytes 524288 | tf_op args[1]
  3.4 143.1 %moe_layer.1 = bf16[128,2048]{1,0:T(8,128)(2,1)} custom-call(s32[128,8]{1,0:T(8,128)} %copy.7.ids_hbm, bf16[2048,64]{1,0:T(8,128)(2,1)} %copy.8.rw_hbm, bf16[128,2048]{1,0:T(8,128)(2,1)} %x_hbm.1, bf16[4,2048,1024]{2,1,0:T(8,128)(2,1)} %wg_hbm.1, bf16[4,2048,1024]{2,1,0:T(8,128)(2,1)} %wu_hbm.1, bf16[4,1024,2048]{2,1,0:T(8,128)(2,1)} %wd_hbm.1), custom_call_target="tpu_custom_call" | custom-call | tf_op jit(solution)/shard_map/moe_layer/pallas_call | solution.py:423
  146.4 1.9 %copy.10 = bf16[128,2048]{1,0:T(8,128)(2,1)} copy(bf16[128,2048]{1,0:T(8,128)(2,1)} %moe_layer.1) | data formatting | bytes 1048576

commit v2 on v1

v2 whole, which is shorter than its diff:
```python
import functools

import jax
import jax.numpy as jnp
from jax import lax
from jax.experimental import pallas as pl
from jax.experimental.pallas import tpu as pltpu
from jax.sharding import PartitionSpec as P

MESH = pl.DeviceIdType.MESH
F32 = jnp.float32
BF16 = jnp.bfloat16

POS = {4: 0, -4: 0, 0: 1, -3: 2, 3: 3, -2: 4, 2: 5, -1: 6, 1: 7}
SIGN = (1, -1)
BACK = ((4, 0), (3, 1), (3, 0), (2, 1), (2, 0), (1, 1), (1, 0))
GU_TILE = 512
DN_TILE = 2048
PIECES = 4


def dot(a, b):
    return jnp.dot(a, b, preferred_element_type=F32)


def layer_kernel(group, ids_hbm, rw_hbm, x_hbm, wg_hbm, wu_hbm, wd_hbm, out_hbm,
                 xg, meta, ids_v, rw_v, tp, xe, hid, eo, cm, part, sib, inb, outv, wgu, wdn,
                 ag_s, ag_r, dx_s, dx_r, mt_s, mt_r, dm_s, dm_r, rs_s, rs_r, sb_s, sb_r,
                 gu_sem, dn_sem, ld_sem, st_sem):
    micro = 64
    half = 32
    piece_rows = micro // PIECES
    me = lax.axis_index('ep')
    core = lax.rem(me, 2)
    other = 1 - core
    nbr = (lax.rem(me + 2, group), lax.rem(me + group - 2, group))
    sibling = me + 1 - 2 * core
    local_experts = wg_hbm.shape[0]
    slots = xe.shape[1] // 4

    def remote(src, dst, ssem, rsem, dev):
        return pltpu.make_async_remote_copy(src_ref=src, dst_ref=dst, send_sem=ssem, recv_sem=rsem,
                                            device_id={'ep': dev}, device_id_type=MESH)

    def gu_copies(e, f):
        cols = pl.ds(f * GU_TILE, GU_TILE)
        return (pltpu.make_async_copy(wg_hbm.at[e, :, cols], wgu.at[f, 0], gu_sem.at[f]),
                pltpu.make_async_copy(wu_hbm.at[e, :, cols], wgu.at[f, 1], gu_sem.at[f]))

    def dn_copy(e, n):
        return pltpu.make_async_copy(wd_hbm.at[e, :, pl.ds(n * DN_TILE, DN_TILE)], wdn.at[n], dn_sem.at[n])

    def x_rows(m, pos, c, start, size):
        row = pl.multiple_of((pos % 2) * 2 * micro + c * micro + start, 16)
        return xg.at[m, pos // 2, pl.ds(row, size)]

    def ag_copy(m, d, k, i):
        start = ((i + d * PIECES // 2) % PIECES) * piece_rows
        src = x_rows(m, POS[-SIGN[d] * k], core, start, piece_rows)
        dst = x_rows(m, POS[-SIGN[d] * (k + 1)], core, start, piece_rows)
        return remote(src, dst, ag_s.at[m, d], ag_r.at[d, k, i], nbr[d])

    def ag_has(k, i):
        return k < 3 or i < PIECES // 2

    def landed(ref, sem):
        pltpu.make_async_copy(ref, ref, sem).wait()

    def dx_copy(m, pos, c):
        ref = x_rows(m, pos, c, 0, micro)
        return remote(ref, ref, dx_s.at[m], dx_r.at[m, pos // 2], sibling)

    def mt_copy(d, k):
        return remote(meta.at[POS[-SIGN[d] * k], core], meta.at[POS[-SIGN[d] * (k + 1)], core],
                      mt_s, mt_r.at[d, k], nbr[d])

    def mt_has(d, k):
        return k < 3 or d == 0

    def dm_copy(pos, c):
        return remote(meta.at[pos, c], meta.at[pos, c], dm_s, dm_r.at[pos // 2], sibling)

    def send_own(m, first, last):
        for i in range(first, last):
            for d in range(2):
                ag_copy(m, d, 0, i).start()
        if last == PIECES:
            dx_copy(m, POS[0], core).start()

    def ag_event(m, k, i):
        for d in range(2):
            ag_copy(m, d, k, i).wait_recv()
            if k < 3 and ag_has(k + 1, i):
                ag_copy(m, d, k + 1, i).start()
        if not ag_has(k, i + 1) or i + 1 == PIECES:
            for pos in ((POS[4],) if k == 3 else (POS[-(k + 1)], POS[k + 1])):
                dx_copy(m, pos, core).start()

    def mt_event(k):
        for d in range(2):
            if mt_has(d, k):
                mt_copy(d, k).wait_recv()
                if k < 3 and mt_has(d, k + 1):
                    mt_copy(d, k + 1).start()
                dm_copy(POS[-SIGN[d] * (k + 1)], core).start()

    def make_meta():
        for m in range(2):
            rows = x_rows(m, POS[0], core, 0, micro)
            tp[m * micro:(m + 1) * micro, 0:rw_v.shape[0]] = lax.dot_general(
                rows[...], rw_v[...], (((1,), (1,)), ((), ())), preferred_element_type=F32)
        ids = ids_v[...].astype(F32)
        expert = lax.broadcasted_iota(jnp.int32, (rw_v.shape[0], 2 * micro), 0).astype(F32)
        logits = tp[...].T[0:rw_v.shape[0]]
        picked = []
        for j in range(8):
            picked.append(jnp.sum(jnp.where(expert == ids[j:j + 1], logits, 0.0), axis=0, keepdims=True))
        picked = jnp.concatenate(picked, axis=0)
        top = jnp.exp(picked - jnp.max(picked, axis=0, keepdims=True))
        gates = top / jnp.sum(top, axis=0, keepdims=True)
        both = jnp.concatenate([ids, gates], axis=0)
        turned = pltpu.roll(both, micro, 1)
        mine = lax.broadcasted_iota(jnp.int32, both.shape, 1) // micro == core
        for m in range(2):
            meta[POS[0], core, m] = jnp.where(mine, jnp.where(core == m, both, turned), 0.0)

    def gather(m, p):
        token = 4 * micro
        info = jnp.concatenate([meta[2 * p, 0, m] + meta[2 * p, 1, m],
                                meta[2 * p + 1, 0, m] + meta[2 * p + 1, 1, m]], axis=1)
        ids, gates = info[0:8], info[8:16]
        chosen, weight = [], []
        for e in range(local_experts):
            hit = ids == (me * local_experts + e).astype(F32)
            chosen.append(jnp.sum(jnp.where(hit, 1.0, 0.0), axis=0, keepdims=True))
            weight.append(jnp.sum(jnp.where(hit, gates, 0.0), axis=0, keepdims=True))
        stacked = jnp.concatenate(chosen + [jnp.zeros((16 - local_experts, token), F32)], axis=0)
        row = lax.broadcasted_iota(jnp.int32, (token, token), 0)
        col = lax.broadcasted_iota(jnp.int32, (token, token), 1)
        before = jnp.where(row < col, 1.0, 0.0).astype(BF16)
        eye = jnp.where(row == col, 1.0, 0.0).astype(BF16)
        rank = dot(stacked.astype(BF16), before)
        slot = lax.broadcasted_iota(jnp.int32, (slots, token), 0).astype(F32)
        pick, mix = [], []
        for e in range(local_experts):
            place = jnp.where(chosen[e] > 0.5, rank[e:e + 1], -1.0)
            at = slot == place
            pick.append(jnp.where(at, 1.0, 0.0))
            mix.append(jnp.where(at, weight[e], 0.0))
        pick = jnp.concatenate(pick, axis=0).astype(BF16)
        rest = jnp.concatenate(mix, axis=0)
        terms = []
        for i in range(3):
            terms.append(rest.astype(BF16))
            rest = rest - terms[i].astype(F32)
        terms = jnp.concatenate(terms, axis=0)
        cm[p] = lax.dot_general(eye, terms, (((1,), (1,)), ((), ())), preferred_element_type=F32).astype(BF16)
        for n in range(0, xg.shape[-1], 512):
            rows = dot(pick, xg[m, p, :, n:n + 512]).astype(BF16)
            for e in range(local_experts):
                xe[e, pl.ds(pl.multiple_of(p * slots, 16), slots), n:n + 512] = rows[e * slots:(e + 1) * slots]

    def experts(first, last, service):
        @pl.loop(first, last)
        def _(e):
            nxt = lax.rem(e + 1, local_experts)

            def after(step):
                for at, fn in service.items():
                    if at[1] == step:
                        pl.when(e == at[0])(fn)

            for f in range(2):
                landed(wgu.at[f], gu_sem.at[f])
                for c in range(0, GU_TILE, 256):
                    a = dot(xe[e], wgu[f, 0, :, c:c + 256])
                    b = dot(xe[e], wgu[f, 1, :, c:c + 256])
                    hid[:, f * GU_TILE + c:f * GU_TILE + c + 256] = (a * jax.nn.sigmoid(a) * b).astype(BF16)
                for cp in gu_copies(nxt, f):
                    cp.start()
                after(f)
            dn_copy(e, 0).wait()
            for c in range(0, DN_TILE, 256):
                o = dot(hid[...], wdn[0, :, c:c + 256]).astype(BF16)
                for p in range(4):
                    eo[p, pl.ds(pl.multiple_of(e * slots, 16), slots), c:c + 256] = o[p * slots:(p + 1) * slots]
            dn_copy(nxt, 0).start()
            after(2)

    def combine(pos):
        p, top = pos // 2, (pos % 2) * 2 * micro
        if not isinstance(pos, int):
            top = pl.multiple_of(top, 2 * micro)
        gates = cm[p, pl.ds(top, 2 * micro)]
        for n in range(0, xg.shape[-1], 512):
            o = eo[p, :, n:n + 512]
            acc = dot(gates, jnp.concatenate([o, o, o], axis=0))
            part[pos, 0, :, n:n + 512] = acc[:micro]
            part[pos, 1, :, n:n + 512] = acc[micro:]

    def sb_copy(m, pos):
        return remote(part.at[pos, other], sib.at[m, pos], sb_s.at[pos], sb_r.at[m, pos], sibling)

    def back_item(d, j):
        dist, rows = BACK[j]
        return POS[SIGN[d] * dist], (rows if d == 0 else 1 - rows)

    def rs_copy(m, d, j):
        pos, r = back_item(d, j)
        return remote(part.at[pos, core, pl.ds(r * half, half)], inb.at[d, j],
                      rs_s.at[pos], rs_r.at[d, j], nbr[d])

    here = set()

    def need_sib(m, pos):
        if (m, pos) not in here:
            here.add((m, pos))
            sb_copy(m, pos).wait_recv()

    def back(m, j):
        for d in range(2):
            pos, r = back_item(d, j)
            need_sib(m, pos)
            rows = pl.ds(r * half, half)
            acc = part[pos, core, rows] + sib[m, pos, rows]
            if j >= 2:
                rs_copy(m, d, j - 2).wait_recv()
                acc = acc + inb[d, j - 2]
            part[pos, core, rows] = acc
            rs_copy(m, d, j).start()

    def st_copy(m, r):
        rows = pl.ds(m * micro + r * half, half)
        return pltpu.make_async_copy(outv.at[rows], out_hbm.at[rows], st_sem)

    def finish(m, r):
        pos = POS[0]
        need_sib(m, pos)
        rows = pl.ds(r * half, half)
        acc = part[pos, core, rows] + sib[m, pos, rows]
        for d in range(2):
            j = 5 if (r == 1) == (d == 0) else 6
            if (m, d, j) not in here:
                here.add((m, d, j))
                rs_copy(m, d, j).wait_recv()
            acc = acc + inb[d, j]
        outv[pl.ds(m * micro + r * half, half)] = acc.astype(BF16)
        st_copy(m, r).start()

    def combine_send(m, pos):
        combine(pos)
        sb_copy(m, pos).start()

    def combine_loop(m, first, last):
        @pl.loop(first, last)
        def _(pos):
            combine_send(m, pos)

    def part_free(m, pos):
        landed(part.at[pos, other], sb_s.at[pos])
        if pos != POS[0]:
            landed(part.at[pos, core], rs_s.at[pos])

    def pair_wait(m, p):
        landed(xg.at[m, p, pl.ds(0, 2 * micro)], dx_r.at[m, p])
        if m == 0:
            landed(meta.at[pl.ds(2 * p, 2), 0], dm_r.at[p])

    loads = [pltpu.make_async_copy(x_hbm.at[pl.ds(m * micro, micro)], x_rows(m, POS[0], core, 0, micro), ld_sem.at[m])
             for m in range(2)]
    loads.append(pltpu.make_async_copy(ids_hbm, ids_v, ld_sem.at[2]))
    loads.append(pltpu.make_async_copy(rw_hbm, rw_v, ld_sem.at[3]))
    for cp in loads:
        cp.start()

    def enter():
        barrier = pltpu.get_barrier_semaphore()
        for dev in (nbr[0], nbr[1], sibling):
            pl.semaphore_signal(barrier, inc=1, device_id={'ep': dev}, device_id_type=MESH)
        pl.semaphore_wait(barrier, 3)

    enter()
    loads[0].wait()

    send_own(0, 0, PIECES // 2)
    for cp in loads[2:]:
        cp.wait()
    loads[1].wait()
    make_meta()
    for d in range(2):
        mt_copy(d, 0).start()
    dm_copy(POS[0], core).start()
    send_own(0, PIECES // 2, PIECES)
    for f in range(2):
        for cp in gu_copies(0, f):
            cp.start()
    dn_copy(0, 0).start()

    for k in range(3):
        for i in range(PIECES):
            ag_event(0, k, i)
            if i == 1:
                mt_event(k)
                if k == 2:
                    send_own(1, 0, PIECES)
        if k == 1:
            pair_wait(0, 3)
            gather(0, 3)
    pair_wait(0, 2)
    gather(0, 2)
    ag_event(0, 3, 0)
    ag_event(0, 3, 1)
    mt_event(3)
    pair_wait(0, 1)
    gather(0, 1)
    pair_wait(0, 0)
    gather(0, 0)

    experts(0, local_experts, {
        (0, 0): lambda: ag_event(1, 0, 0),
        (0, 1): lambda: ag_event(1, 0, 1),
        (0, 2): lambda: ag_event(1, 0, 2),
        (1, 1): lambda: ag_event(1, 0, 3),
        (1, 2): lambda: ag_event(1, 1, 0),
        (2, 0): lambda: ag_event(1, 1, 1),
        (2, 2): lambda: ag_event(1, 1, 2),
        (3, 0): lambda: ag_event(1, 1, 3),
        (3, 2): lambda: ag_event(1, 2, 0),
    })
    combine_send(0, 0)
    ag_event(1, 2, 1)
    combine_loop(0, 2, 4)
    ag_event(1, 2, 2)
    ag_event(1, 2, 3)
    back(0, 0)
    back(0, 1)
    combine_loop(0, 4, 8)
    combine_send(0, 1)
    ag_event(1, 3, 0)
    ag_event(1, 3, 1)
    for p in range(4):
        pair_wait(1, p)

    @pl.loop(0, 4)
    def _(p):
        gather(1, p)

    for j in range(2, 7):
        for d in range(2):
            need_sib(0, back_item(d, j)[0])

    experts(0, local_experts, {
        (1, 0): lambda: back(0, 2),
        (2, 2): lambda: back(0, 3),
    })
    back(0, 4)
    part_free(0, 0)
    combine_send(1, 0)
    part_free(0, 2)
    part_free(0, 3)
    combine_loop(1, 2, 4)
    back(0, 5)
    back(0, 6)
    back(1, 0)
    back(1, 1)
    finish(0, 0)
    finish(0, 1)
    for pos in (4, 5, 6, 7, 1):
        part_free(0, pos)
    combine_loop(1, 4, 8)
    combine_send(1, 1)
    for j in range(2, 7):
        back(1, j)
    finish(1, 0)
    finish(1, 1)

    def drain():
        for m in range(2):
            for d in range(2):
                landed(xg.at[m, 0, pl.ds(0, (3 * PIECES + PIECES // 2) * piece_rows)], ag_s.at[m, d])
            landed(xg.at[m, pl.ds(0, 2)], dx_s.at[m])
        landed(meta.at[pl.ds(0, 7), 0], mt_s)
        landed(meta.at[pl.ds(0, 8), 0], dm_s)
        for pos in range(8):
            part_free(1, pos)
        for f in range(2):
            landed(wgu.at[f], gu_sem.at[f])
        dn_copy(0, 0).wait()
        landed(outv, st_sem)

    drain()


def solution(mesh):
    group = mesh.shape['ep']

    def device_fn(act_in, router_w, expert_ids, w_gate, w_up, w_down):
        tokens, dim = act_in.shape
        local_experts, _, ffn = w_gate.shape
        micro = tokens // 2
        half = micro // 2
        mean_load = micro * expert_ids.shape[1] // (local_experts * group)
        cap = mean_load + mean_load // 2
        slots = 4 * cap
        dma = pltpu.SemaphoreType.DMA
        scratch = [
            pltpu.VMEM((2, 4, 4 * micro, dim), BF16),
            pltpu.VMEM((8, 2, 2, 16, 2 * micro), F32),
            pltpu.VMEM(expert_ids.shape[::-1], jnp.int32),
            pltpu.VMEM(router_w.shape[::-1], BF16),
            pltpu.VMEM((tokens, 128), F32),
            pltpu.VMEM((local_experts, 4 * slots, dim), BF16),
            pltpu.VMEM((4 * slots, ffn), BF16),
            pltpu.VMEM((4, local_experts * slots, dim), BF16),
            pltpu.VMEM((4, 4 * micro, 3 * local_experts * slots), BF16),
            pltpu.VMEM((8, 2, micro, dim), F32),
            pltpu.VMEM((2, 8, micro, dim), F32),
            pltpu.VMEM((2, 7, half, dim), F32),
            pltpu.VMEM((tokens, dim), BF16),
            pltpu.VMEM((2, 2, dim, GU_TILE), BF16),
            pltpu.VMEM((1, ffn, DN_TILE), BF16),
            dma((2, 2)), dma((2, 4, PIECES)),
            dma((2,)), dma((2, 4)),
            dma, dma((2, 4)),
            dma, dma((4,)),
            dma((8,)), dma((2, 7)),
            dma((8,)), dma((2, 8)),
            dma((2,)), dma((1,)), dma((4,)), dma,
        ]
        return pl.pallas_call(
            functools.partial(layer_kernel, group),
            out_shape=jax.ShapeDtypeStruct((tokens, dim), BF16),
            in_specs=[pl.BlockSpec(memory_space=pl.ANY)] * 6,
            out_specs=pl.BlockSpec(memory_space=pl.ANY),
            scratch_shapes=scratch,
            compiler_params=pltpu.CompilerParams(collective_id=0, has_side_effects=True,
                                                 vmem_limit_bytes=67043328),
            name='moe_layer',
        )(expert_ids.T, router_w.T, act_in, w_gate, w_up, w_down)

    row_spec = P(('dp', 'ep'), None)
    expert_spec = P('ep', None, None)
    return jax.shard_map(device_fn, mesh=mesh,
                         in_specs=(row_spec, P(None, None), row_spec, expert_spec, expert_spec, expert_spec),
                         out_specs=row_spec, check_vma=False)
```

time: 149 us -> 139 us (0.933)
  Pallas kernels: 143 us -> 137 us
  local copies, waits for them, and re-layouts: 5.24 us -> 1.88 us
    pallas_call x1, Pallas kernels: 143 us -> 137 us  [device_fn(): pl.pallas_call(functools.partial(layer_kernel, group), out_shape=jax.Shap...]
    unnamed x3 -> x1, local copies, waits for them, and re-layouts: 5.24 us -> 1.88 us
where the time goes in v2:
time: 139 us
  Pallas kernels  137 us (99%)
  local copies, waits for them, and re-layouts  1.88 us (1%)
    pallas_call x1, Pallas kernels, device_fn(): pl.pallas_call(functools.partial(layer_kernel, group), out_shape=jax.Shap...  137 us

profile of v2, /device:TPU:21, one launch (start us, length us, event | category | flops | bytes accessed | tf_op | source)
XLA Modules:
  0.0 138.8 jit_solution(3505582332423061309)
XLA Ops:
  0.0 136.9 %moe_layer.1 = bf16[128,2048]{1,0:T(8,128)(2,1)} custom-call(s32[8,128]{1,0:T(8,128)} %bitcast.3, bf16[64,2048]{1,0:T(8,128)(2,1)} %bitcast.2, bf16[128,2048]{1,0:T(8,128)(2,1)} %x_hbm.1, bf16[4,2048,1024]{2,1,0:T(8,128)(2,1)} %wg_hbm.1, bf16[4,2048,1024]{2,1,0:T(8,128)(2,1)} %wu_hbm.1, bf16[4,1024,2048]{2,1,0:T(8,128)(2,1)} %wd_hbm.1), custom_call_target="tpu_custom_call" | custom-call | tf_op jit(solution)/shard_map/moe_layer/pallas_call | solution.py:430
  136.9 1.9 %copy.8 = bf16[128,2048]{1,0:T(8,128)(2,1)} copy(bf16[128,2048]{1,0:T(8,128)(2,1)} %moe_layer.1) | data formatting | bytes 1048576

commit v3 on v2

v3 whole, which is shorter than its diff:
```python
import functools

import jax
import jax.numpy as jnp
from jax import lax
from jax.experimental import pallas as pl
from jax.experimental.pallas import tpu as pltpu
from jax.sharding import PartitionSpec as P

MESH = pl.DeviceIdType.MESH
F32 = jnp.float32
BF16 = jnp.bfloat16

FAR = 4
ORDER = (FAR, 0, -3, 3, -2, 2, -1, 1)
POS = {away: i for i, away in enumerate(ORDER)}
POS[-FAR] = POS[FAR]
HERE = POS[0]
CHIPS = len(ORDER)
PAIRS = CHIPS // 2
SIGN = (1, -1)
TERMS = 3
NT = (((1,), (1,)), ((), ()))
BACK = ((FAR, 0),) + tuple((away, r) for away in range(FAR - 1, 0, -1) for r in (1, 0))
SENDS = len(BACK)
STEPS = 3
GU_TILE = 512
WIDE = 512
MXU = 256
PIECES = 4


def dot(a, b):
    return jnp.dot(a, b, preferred_element_type=F32)


def layer_kernel(group, ids_hbm, rw_hbm, x_hbm, wg_hbm, wu_hbm, wd_hbm, out_hbm,
                 xg, meta, ids_v, rw_v, tp, xe, hid, eo, picks, cm, part, sib, inb, outv, wgu, wdn,
                 ag_s, ag_r, dx_s, dx_r, mt_s, mt_r, dm_s, dm_r, rs_s, rs_r, sb_s, sb_r,
                 gu_sem, dn_sem, ld_sem, st_sem):
    micro = outv.shape[0] // 2
    chip = 2 * micro
    half = micro // 2
    dim = outv.shape[1]
    last = FAR - 1
    piece_rows = micro // PIECES
    me = lax.axis_index('ep')
    core = lax.rem(me, 2)
    other = 1 - core
    nbr = (lax.rem(me + 2, group), lax.rem(me + group - 2, group))
    sibling = me + 1 - 2 * core
    local_experts = wg_hbm.shape[0]
    slots = xe.shape[1] // 4

    def remote(src, dst, ssem, rsem, dev):
        return pltpu.make_async_remote_copy(src_ref=src, dst_ref=dst, send_sem=ssem, recv_sem=rsem,
                                            device_id={'ep': dev}, device_id_type=MESH)

    def gu_copies(e, f):
        cols = pl.ds(f * GU_TILE, GU_TILE)
        s = lax.rem(e, 2)
        return (pltpu.make_async_copy(wg_hbm.at[e, :, cols], wgu.at[s, f, 0], gu_sem.at[s, f]),
                pltpu.make_async_copy(wu_hbm.at[e, :, cols], wgu.at[s, f, 1], gu_sem.at[s, f]))

    def dn_copy(e):
        return pltpu.make_async_copy(wd_hbm.at[e], wdn.at[lax.rem(e, 2)], dn_sem.at[lax.rem(e, 2)])

    def load_weights():
        for e in range(2):
            for f in range(2):
                for cp in gu_copies(e, f):
                    cp.start()
            dn_copy(e).start()

    def x_rows(m, pos, c, start, size):
        row = pl.multiple_of((pos % 2) * chip + c * micro + start, 16)
        return xg.at[m, pos // 2, pl.ds(row, size)]

    def ag_copy(m, d, k, i):
        start = ((i + d * PIECES // 2) % PIECES) * piece_rows
        src = x_rows(m, POS[-SIGN[d] * k], core, start, piece_rows)
        dst = x_rows(m, POS[-SIGN[d] * (k + 1)], core, start, piece_rows)
        return remote(src, dst, ag_s.at[m, d], ag_r.at[d, k, i], nbr[d])

    def ag_has(k, i):
        return k < last or i < PIECES // 2

    def landed(ref, sem):
        pltpu.make_async_copy(ref, ref, sem).wait()

    def dx_copy(m, pos, c):
        ref = x_rows(m, pos, c, 0, micro)
        return remote(ref, ref, dx_s.at[m], dx_r.at[m, pos // 2], sibling)

    def mt_copy(d, k):
        return remote(meta.at[POS[-SIGN[d] * k], core], meta.at[POS[-SIGN[d] * (k + 1)], core],
                      mt_s, mt_r.at[d, k], nbr[d])

    def mt_has(d, k):
        return k < last or d == 0

    def dm_copy(pos, c):
        return remote(meta.at[pos, c], meta.at[pos, c], dm_s, dm_r.at[pos // 2], sibling)

    def send_own(m, first, last):
        for i in range(first, last):
            for d in range(2):
                ag_copy(m, d, 0, i).start()
        if last == PIECES:
            dx_copy(m, HERE, core).start()

    def ag_event(m, k, i):
        for d in range(2):
            ag_copy(m, d, k, i).wait_recv()
            if k < last and ag_has(k + 1, i):
                ag_copy(m, d, k + 1, i).start()
        if k == last:
            for d in range(2):
                ref = x_rows(m, POS[FAR], core, (i + d * PIECES // 2) * piece_rows, piece_rows)
                remote(ref, ref, dx_s.at[m], dx_r.at[m, POS[FAR] // 2], sibling).start()
        elif i + 1 == PIECES:
            for d in range(2):
                dx_copy(m, POS[-SIGN[d] * (k + 1)], core).start()

    def take(m, first, after):
        for n in range(first, after):
            ag_event(m, n // PIECES, n % PIECES)

    def mt_event(k):
        for d in range(2):
            if mt_has(d, k):
                mt_copy(d, k).wait_recv()
                if k < last and mt_has(d, k + 1):
                    mt_copy(d, k + 1).start()
                dm_copy(POS[-SIGN[d] * (k + 1)], core).start()

    def make_meta():
        for m in range(2):
            rows = x_rows(m, HERE, core, 0, micro)
            tp[m * micro:(m + 1) * micro, 0:rw_v.shape[0]] = lax.dot_general(
                rows[...], rw_v[...], NT, preferred_element_type=F32)
        ids = ids_v[...].astype(F32)
        expert = lax.broadcasted_iota(jnp.int32, (rw_v.shape[0], chip), 0).astype(F32)
        logits = tp[...].T[0:rw_v.shape[0]]
        picked = []
        for j in range(8):
            picked.append(jnp.sum(jnp.where(expert == ids[j:j + 1], logits, 0.0), axis=0, keepdims=True))
        picked = jnp.concatenate(picked, axis=0)
        top = jnp.exp(picked - jnp.max(picked, axis=0, keepdims=True))
        gates = top / jnp.sum(top, axis=0, keepdims=True)
        both = jnp.concatenate([ids, gates], axis=0)
        turned = pltpu.roll(both, micro, 1)
        mine = lax.broadcasted_iota(jnp.int32, both.shape, 1) // micro == core
        for m in range(2):
            meta[HERE, core, m] = jnp.where(mine, jnp.where(core == m, both, turned), 0.0)

    def index(m, p):
        token = 2 * chip
        info = jnp.concatenate([meta[2 * p, 0, m] + meta[2 * p, 1, m],
                                meta[2 * p + 1, 0, m] + meta[2 * p + 1, 1, m]], axis=1)
        ids, gates = info[0:8], info[8:16]
        chosen, weight = [], []
        for e in range(local_experts):
            hit = ids == (me * local_experts + e).astype(F32)
            chosen.append(jnp.sum(jnp.where(hit, 1.0, 0.0), axis=0, keepdims=True))
            weight.append(jnp.sum(jnp.where(hit, gates, 0.0), axis=0, keepdims=True))
        stacked = jnp.concatenate(chosen + [jnp.zeros((16 - local_experts, token), F32)], axis=0)
        row = lax.broadcasted_iota(jnp.int32, (token, token), 0)
        col = lax.broadcasted_iota(jnp.int32, (token, token), 1)
        before = jnp.where(row < col, 1.0, 0.0).astype(BF16)
        eye = jnp.where(row == col, 1.0, 0.0).astype(BF16)
        rank = dot(stacked.astype(BF16), before)
        slot = lax.broadcasted_iota(jnp.int32, (slots, token), 0).astype(F32)
        pick, mix = [], []
        for e in range(local_experts):
            place = jnp.where(chosen[e] > 0.5, rank[e:e + 1], -1.0)
            at = slot == place
            pick.append(jnp.where(at, 1.0, 0.0))
            mix.append(jnp.where(at, weight[e], 0.0))
        picks[m, p] = jnp.concatenate(pick, axis=0).astype(BF16)
        rest = jnp.concatenate(mix, axis=0)
        terms = []
        for i in range(TERMS):
            terms.append(rest.astype(BF16))
            rest = rest - terms[i].astype(F32)
        terms = jnp.concatenate(terms, axis=0)
        cm[m, p] = lax.dot_general(eye, terms, NT, preferred_element_type=F32).astype(BF16)

    def gather(m, p):
        for n in range(0, dim, WIDE):
            rows = dot(picks[m, p], xg[m, p, :, n:n + WIDE]).astype(BF16)
            for e in range(local_experts):
                xe[e, pl.ds(pl.multiple_of(p * slots, 16), slots), n:n + WIDE] = rows[e * slots:(e + 1) * slots]

    def experts(m, service):
        @pl.loop(0, local_experts)
        def _(e):
            s = lax.rem(e, 2)
            nxt = lax.rem(e + 2, local_experts)

            def after(step, copies):
                def start():
                    for cp in copies:
                        cp.start()

                if m == 0:
                    start()
                else:
                    pl.when(e + 2 < local_experts)(start)
                for at, fn in service.items():
                    if at[1] == step:
                        who = functools.reduce(lambda x, c: x & (core == c), at[2:], e == at[0])
                        pl.when(who)(fn)

            for f in range(2):
                landed(wgu.at[s, f], gu_sem.at[s, f])
                for c in range(0, GU_TILE, MXU):
                    a = dot(xe[e], wgu[s, f, 0, :, c:c + MXU])
                    b = dot(xe[e], wgu[s, f, 1, :, c:c + MXU])
                    hid[:, f * GU_TILE + c:f * GU_TILE + c + MXU] = (a * jax.nn.sigmoid(a) * b).astype(BF16)
                after(f, gu_copies(nxt, f))
            dn_copy(e).wait()
            for c in range(0, dim, MXU):
                o = dot(hid[...], wdn[s, :, c:c + MXU]).astype(BF16)
                for p in range(4):
                    eo[p, pl.ds(pl.multiple_of(e * slots, 16), slots), c:c + MXU] = o[p * slots:(p + 1) * slots]
            after(2, (dn_copy(nxt),))

    def combine(m, pos):
        p, top = pos // 2, (pos % 2) * chip
        if not isinstance(pos, int):
            top = pl.multiple_of(top, chip)
        gates = cm[m, p, pl.ds(top, chip)]
        for n in range(0, dim, WIDE):
            o = eo[p, :, n:n + WIDE]
            acc = dot(gates, jnp.concatenate([o, o, o], axis=0))
            part[pos, 0, :, n:n + WIDE] = acc[:micro]
            part[pos, 1, :, n:n + WIDE] = acc[micro:]

    def sb_copy(m, pos):
        return remote(part.at[pos, other], sib.at[m, pos], sb_s.at[pos], sb_r.at[m, pos], sibling)

    def back_item(d, j):
        dist, rows = BACK[j]
        return POS[SIGN[d] * dist], (rows if d == 0 else 1 - rows)

    def rs_copy(m, d, j):
        pos, r = back_item(d, j)
        return remote(part.at[pos, core, pl.ds(r * half, half)], inb.at[d, j],
                      rs_s.at[pos], rs_r.at[d, j], nbr[d])

    seen = set()

    def need_sib(m, pos):
        if (m, pos) not in seen:
            seen.add((m, pos))
            sb_copy(m, pos).wait_recv()

    def back(m, j):
        for d in range(2):
            pos, r = back_item(d, j)
            need_sib(m, pos)
            rows = pl.ds(r * half, half)
            acc = part[pos, core, rows] + sib[m, pos, rows]
            if j >= 2:
                rs_copy(m, d, j - 2).wait_recv()
                acc = acc + inb[d, j - 2]
            part[pos, core, rows] = acc
            rs_copy(m, d, j).start()

    def st_copy(m, r):
        rows = pl.ds(m * micro + r * half, half)
        return pltpu.make_async_copy(outv.at[rows], out_hbm.at[rows], st_sem)

    def finish(m, r):
        pos = HERE
        need_sib(m, pos)
        rows = pl.ds(r * half, half)
        acc = part[pos, core, rows] + sib[m, pos, rows]
        for d in range(2):
            j = 5 if (r == 1) == (d == 0) else 6
            if (m, d, j) not in seen:
                seen.add((m, d, j))
                rs_copy(m, d, j).wait_recv()
            acc = acc + inb[d, j]
        outv[pl.ds(m * micro + r * half, half)] = acc.astype(BF16)
        st_copy(m, r).start()

    def combine_send(m, pos):
        combine(m, pos)
        sb_copy(m, pos).start()

    def combine_loop(m, first, last):
        @pl.loop(first, last)
        def _(pos):
            combine_send(m, pos)

    def part_free(m, pos):
        landed(part.at[pos, other], sb_s.at[pos])
        if pos != HERE:
            landed(part.at[pos, core], rs_s.at[pos])

    def pair_wait(m, p):
        landed(xg.at[m, p, pl.ds(0, chip)], dx_r.at[m, p])

    def info_wait(p):
        landed(meta.at[pl.ds(2 * p, 2), 0], dm_r.at[p])

    loads = [pltpu.make_async_copy(x_hbm.at[pl.ds(m * micro, micro)], x_rows(m, HERE, core, 0, micro), ld_sem.at[m])
             for m in range(2)]
    loads.append(pltpu.make_async_copy(ids_hbm, ids_v, ld_sem.at[2]))
    loads.append(pltpu.make_async_copy(rw_hbm, rw_v, ld_sem.at[3]))
    for cp in loads:
        cp.start()

    def enter():
        barrier = pltpu.get_barrier_semaphore()
        for dev in (nbr[0], nbr[1], sibling):
            pl.semaphore_signal(barrier, inc=1, device_id={'ep': dev}, device_id_type=MESH)
        pl.semaphore_wait(barrier, 3)

    enter()
    loads[0].wait()

    send_own(0, 0, 1)
    for cp in loads[2:]:
        cp.wait()
    loads[1].wait()
    make_meta()
    for d in range(2):
        mt_copy(d, 0).start()
    dm_copy(HERE, core).start()
    send_own(0, 1, PIECES)
    load_weights()

    def prepare(p):
        info_wait(p)
        index(0, p)

    def fetch(m, p):
        pair_wait(m, p)
        gather(m, p)

    near, mid, wide, far = 3, 2, 1, 0
    for k in range(last - 1):
        mt_event(k)
        take(0, k * PIECES, (k + 1) * PIECES)
    prepare(near)
    pair_wait(0, near)
    mt_event(last - 1)
    n = (last - 1) * PIECES
    take(0, n, n + 1)
    gather(0, near)
    take(0, n + 1, n + 2)
    send_own(1, 0, PIECES)
    index(1, near)
    take(0, n + 2, n + 3)
    prepare(mid)
    take(0, n + 3, n + PIECES)
    fetch(0, mid)
    n = last * PIECES
    mt_event(last)
    prepare(wide)
    take(0, n, n + 1)
    prepare(far)
    take(0, n + 1, n + 2)
    pl.when(core == 1)(functools.partial(take, 1, 0, 1))
    fetch(0, wide)
    fetch(0, far)
    pl.when(core == 1)(functools.partial(take, 1, 1, 2))

    due = {}
    for c, first, steps in ((0, 0, (0, 1, 3, 4, 6, 7, 9, 10, 11)), (1, 2, (0, 2, 3, 4, 6, 7, 8, 10))):
        for n, step in enumerate(steps, first):
            due[divmod(step, STEPS) + (c,)] = functools.partial(take, 1, n, n + 1)
    experts(0, due)
    combine_send(0, 0)
    n = (last - 1) * PIECES + 1
    pl.when(core == 0)(functools.partial(take, 1, n, n + 1))
    combine_loop(0, 2, FAR)
    back(0, 0)
    take(1, n + 1, last * PIECES)
    back(0, 1)
    combine_loop(0, FAR, FAR + 2)
    take(1, last * PIECES, last * PIECES + 2)
    combine_loop(0, FAR + 2, CHIPS)
    combine_send(0, HERE)
    for p in range(near):
        index(1, p)
    for p in range(PAIRS):
        fetch(1, p)

    for j in range(2, SENDS):
        for d in range(2):
            need_sib(0, back_item(d, j)[0])

    experts(1, {
        (0, 2): functools.partial(back, 0, 2),
        (2, 2): functools.partial(back, 0, 3),
    })
    part_free(0, 0)
    combine_send(1, 0)
    back(0, 4)
    part_free(0, 2)
    part_free(0, 3)
    combine_loop(1, 2, FAR)
    back(0, 5)
    back(0, 6)
    back(1, 0)
    back(1, 1)
    finish(0, 0)
    finish(0, 1)
    for pos in (HERE, *range(FAR, CHIPS)):
        part_free(0, pos)
    combine_loop(1, FAR, CHIPS)
    combine_send(1, HERE)
    for j in range(2, SENDS):
        back(1, j)
    finish(1, 0)
    finish(1, 1)

    def drain():
        for m in range(2):
            for d in range(2):
                landed(xg.at[m, 0, pl.ds(0, (3 * PIECES + PIECES // 2) * piece_rows)], ag_s.at[m, d])
            landed(xg.at[m, pl.ds(0, 2)], dx_s.at[m])
        landed(meta.at[pl.ds(0, 7), 0], mt_s)
        landed(meta.at[pl.ds(0, 8), 0], dm_s)
        for pos in range(CHIPS):
            part_free(1, pos)
        landed(outv, st_sem)

    drain()


def solution(mesh):
    group = mesh.shape['ep']

    def device_fn(act_in, router_w, expert_ids, w_gate, w_up, w_down):
        tokens, dim = act_in.shape
        local_experts, _, ffn = w_gate.shape
        micro = tokens // 2
        half = micro // 2
        mean_load = micro * expert_ids.shape[1] // (local_experts * group)
        cap = mean_load + mean_load // 2
        slots = 4 * cap
        dma = pltpu.SemaphoreType.DMA
        scratch = [
            pltpu.VMEM((2, 4, 4 * micro, dim), BF16),
            pltpu.VMEM((8, 2, 2, 16, 2 * micro), F32),
            pltpu.VMEM(expert_ids.shape[::-1], jnp.int32),
            pltpu.VMEM(router_w.shape[::-1], BF16),
            pltpu.VMEM((tokens, 128), F32),
            pltpu.VMEM((local_experts, 4 * slots, dim), BF16),
            pltpu.VMEM((4 * slots, ffn), BF16),
            pltpu.VMEM((4, local_experts * slots, dim), BF16),
            pltpu.VMEM((2, 4, local_experts * slots, 4 * micro), BF16),
            pltpu.VMEM((2, 4, 4 * micro, 3 * local_experts * slots), BF16),
            pltpu.VMEM((8, 2, micro, dim), F32),
            pltpu.VMEM((2, 8, micro, dim), F32),
            pltpu.VMEM((2, 7, half, dim), F32),
            pltpu.VMEM((tokens, dim), BF16),
            pltpu.VMEM((2, 2, 2, dim, GU_TILE), BF16),
            pltpu.VMEM((2, ffn, dim), BF16),
            dma((2, 2)), dma((2, 4, PIECES)),
            dma((2,)), dma((2, 4)),
            dma, dma((2, 4)),
            dma, dma((4,)),
            dma((8,)), dma((2, 7)),
            dma((8,)), dma((2, 8)),
            dma((2, 2)), dma((2,)), dma((4,)), dma,
        ]
        return pl.pallas_call(
            functools.partial(layer_kernel, group),
            out_shape=jax.ShapeDtypeStruct((tokens, dim), BF16),
            in_specs=[pl.BlockSpec(memory_space=pl.ANY)] * 6,
            out_specs=pl.BlockSpec(memory_space=pl.ANY),
            scratch_shapes=scratch,
            compiler_params=pltpu.CompilerParams(collective_id=0, has_side_effects=True,
                                                 vmem_limit_bytes=67043328),
            name='moe_layer',
        )(expert_ids.T, router_w.T, act_in, w_gate, w_up, w_down)

    row_spec = P(('dp', 'ep'), None)
    expert_spec = P('ep', None, None)
    return jax.shard_map(device_fn, mesh=mesh,
                         in_specs=(row_spec, P(None, None), row_spec, expert_spec, expert_spec, expert_spec),
                         out_specs=row_spec, check_vma=False)
```

time: 139 us -> 133 us (0.957)
  Pallas kernels: 137 us -> 131 us
    pallas_call x1, Pallas kernels: 137 us -> 131 us  [device_fn(): pl.pallas_call(functools.partial(layer_kernel, group), out_shape=jax.Shap...]
where the time goes in v3:
time: 133 us
  Pallas kernels  131 us (98%)
  local copies, waits for them, and re-layouts  1.88 us (1%)
    pallas_call x1, Pallas kernels, device_fn(): pl.pallas_call(functools.partial(layer_kernel, group), out_shape=jax.Shap...  131 us

profile of v3, /device:TPU:21, one launch (start us, length us, event | category | flops | bytes accessed | tf_op | source)
XLA Modules:
  0.0 132.9 jit_solution(4524841611515620007)
XLA Ops:
  0.0 131.0 %moe_layer.1 = bf16[128,2048]{1,0:T(8,128)(2,1)} custom-call(s32[8,128]{1,0:T(8,128)} %bitcast.3, bf16[64,2048]{1,0:T(8,128)(2,1)} %bitcast.2, bf16[128,2048]{1,0:T(8,128)(2,1)} %x_hbm.1, bf16[4,2048,1024]{2,1,0:T(8,128)(2,1)} %wg_hbm.1, bf16[4,2048,1024]{2,1,0:T(8,128)(2,1)} %wu_hbm.1, bf16[4,1024,2048]{2,1,0:T(8,128)(2,1)} %wd_hbm.1), custom_call_target="tpu_custom_call" | custom-call | tf_op jit(solution)/shard_map/moe_layer/pallas_call | solution.py:473
  131.0 1.9 %copy.8 = bf16[128,2048]{1,0:T(8,128)(2,1)} copy(bf16[128,2048]{1,0:T(8,128)(2,1)} %moe_layer.1) | data formatting | bytes 1048576

commit v4 on v3

--- a/solution.py
+++ b/solution.py
@@ -35,13 +35,13 @@
 
 
 def layer_kernel(group, ids_hbm, rw_hbm, x_hbm, wg_hbm, wu_hbm, wd_hbm, out_hbm,
-                 xg, meta, ids_v, rw_v, tp, xe, hid, eo, picks, cm, part, sib, inb, outv, wgu, wdn,
+                 xg, meta, ids_v, rw_v, tp, xe, hid, eo, picks, cm, fm, rows_out, rows_sib, rows_in, part, sib, inb, outv, wgu, wdn,
                  ag_s, ag_r, dx_s, dx_r, mt_s, mt_r, dm_s, dm_r, rs_s, rs_r, sb_s, sb_r,
                  gu_sem, dn_sem, ld_sem, st_sem):
     micro = outv.shape[0] // 2
     chip = 2 * micro
-    half = micro // 2
     dim = outv.shape[1]
+    half = dim // 2
     last = FAR - 1
     piece_rows = micro // PIECES
     me = lax.axis_index('ep')
@@ -50,7 +50,8 @@
     nbr = (lax.rem(me + 2, group), lax.rem(me + group - 2, group))
     sibling = me + 1 - 2 * core
     local_experts = wg_hbm.shape[0]
-    slots = xe.shape[1] // 4
+    slots = xe.shape[1] // PAIRS
+    cap = slots // (2 * 2)
 
     def remote(src, dst, ssem, rsem, dev):
         return pltpu.make_async_remote_copy(src_ref=src, dst_ref=dst, send_sem=ssem, recv_sem=rsem,
@@ -154,37 +155,57 @@
         for m in range(2):
             meta[HERE, core, m] = jnp.where(mine, jnp.where(core == m, both, turned), 0.0)
 
-    def index(m, p):
-        token = 2 * chip
-        info = jnp.concatenate([meta[2 * p, 0, m] + meta[2 * p, 1, m],
-                                meta[2 * p + 1, 0, m] + meta[2 * p + 1, 1, m]], axis=1)
+    def grid(shape, axis):
+        return lax.broadcasted_iota(jnp.int32, shape, axis)
+
+    def one(mask):
+        return jnp.where(mask, 1.0, 0.0).astype(BF16)
+
+    def chip_info(pos, m):
+        return meta[pos, 0, m] + meta[pos, 1, m]
+
+    def places(info, first, count):
+        token = info.shape[1]
         ids, gates = info[0:8], info[8:16]
         chosen, weight = [], []
-        for e in range(local_experts):
-            hit = ids == (me * local_experts + e).astype(F32)
+        for e in range(count):
+            hit = ids == (first + e).astype(F32)
             chosen.append(jnp.sum(jnp.where(hit, 1.0, 0.0), axis=0, keepdims=True))
             weight.append(jnp.sum(jnp.where(hit, gates, 0.0), axis=0, keepdims=True))
-        stacked = jnp.concatenate(chosen + [jnp.zeros((16 - local_experts, token), F32)], axis=0)
-        row = lax.broadcasted_iota(jnp.int32, (token, token), 0)
-        col = lax.broadcasted_iota(jnp.int32, (token, token), 1)
-        before = jnp.where(row < col, 1.0, 0.0).astype(BF16)
-        eye = jnp.where(row == col, 1.0, 0.0).astype(BF16)
-        rank = dot(stacked.astype(BF16), before)
-        slot = lax.broadcasted_iota(jnp.int32, (slots, token), 0).astype(F32)
-        pick, mix = [], []
-        for e in range(local_experts):
-            place = jnp.where(chosen[e] > 0.5, rank[e:e + 1], -1.0)
-            at = slot == place
-            pick.append(jnp.where(at, 1.0, 0.0))
-            mix.append(jnp.where(at, weight[e], 0.0))
-        picks[m, p] = jnp.concatenate(pick, axis=0).astype(BF16)
-        rest = jnp.concatenate(mix, axis=0)
+        stacked = jnp.concatenate(chosen + [jnp.zeros((info.shape[0] - count, token), F32)], axis=0)
+        row, col = grid((token, token), 0), grid((token, token), 1)
+        rank = dot(stacked.astype(BF16), one((row < col) & (row // micro == col // micro)))
+        return [jnp.where(chosen[e] > 0.5, rank[e:e + 1], -slots) for e in range(count)], weight, one(row == col)
+
+    def three_terms(rest):
         terms = []
         for i in range(TERMS):
             terms.append(rest.astype(BF16))
             rest = rest - terms[i].astype(F32)
-        terms = jnp.concatenate(terms, axis=0)
-        cm[m, p] = lax.dot_general(eye, terms, NT, preferred_element_type=F32).astype(BF16)
+        return jnp.concatenate(terms, axis=0)
+
+    def index(m, p):
+        info = jnp.concatenate([chip_info(2 * p, m), chip_info(2 * p + 1, m)], axis=1)
+        place, weight, eye = places(info, me * local_experts, local_experts)
+        slot = grid((slots, 2 * chip), 0) - grid((slots, 2 * chip), 1) // micro * cap
+        slot = slot.astype(F32)
+        at = [slot == place[e] for e in range(local_experts)]
+        picks[m, p] = jnp.concatenate([jnp.where(a, 1.0, 0.0) for a in at], axis=0).astype(BF16)
+        mix = jnp.concatenate([jnp.where(at[e], weight[e], 0.0) for e in range(local_experts)], axis=0)
+        cm[m, p] = lax.dot_general(eye, three_terms(mix), NT, preferred_element_type=F32).astype(BF16)
+
+    def index_far(m, d):
+        count = 2 * local_experts
+        home = POS[SIGN[d] * (FAR - 1)]
+        first = lax.rem(me - core + group - 2 * SIGN[d], group) * local_experts
+        place, weight, eye = places(chip_info(home, m), first, count)
+        slot = grid((16, chip), 0).astype(F32)
+        mix = jnp.concatenate([jnp.where(slot == place[e], weight[e], 0.0) for e in range(count)], axis=0)
+        turned = lax.dot_general(eye, three_terms(mix), NT, preferred_element_type=F32).astype(BF16)
+        wide, tight = 16 * count, cap * count
+        row, col = grid((TERMS * wide, TERMS * tight), 0), grid((TERMS * wide, TERMS * tight), 1)
+        i = col % tight
+        fm[m, d] = dot(turned, one((row // wide == col // tight) & (row % wide == i // cap * 16 + i % cap))).astype(BF16)
 
     def gather(m, p):
         for n in range(0, dim, WIDE):
@@ -234,57 +255,80 @@
         for n in range(0, dim, WIDE):
             o = eo[p, :, n:n + WIDE]
             acc = dot(gates, jnp.concatenate([o, o, o], axis=0))
-            part[pos, 0, :, n:n + WIDE] = acc[:micro]
-            part[pos, 1, :, n:n + WIDE] = acc[micro:]
+            part[pos - 1, 0, :, n:n + WIDE] = acc[:micro]
+            part[pos - 1, 1, :, n:n + WIDE] = acc[micro:]
+
+    def far_rows(m):
+        count = local_experts * cap
+        shape = (2 * count, local_experts * slots)
+        row, col = grid(shape, 0), grid(shape, 1)
+        i = row % count
+        owner = jnp.where(row < count, core, other)
+        take_row = one(col == i // cap * slots + owner * cap + i % cap)
+        for n in range(0, dim, WIDE):
+            o = dot(take_row, eo[0, :, n:n + WIDE]).astype(BF16)
+            rows_out[m, core, :, n:n + WIDE] = o[:count]
+            rows_sib[:, n:n + WIDE] = o[count:]
+        sb_copy(m, 0).start()
 
     def sb_copy(m, pos):
-        return remote(part.at[pos, other], sib.at[m, pos], sb_s.at[pos], sb_r.at[m, pos], sibling)
+        if isinstance(pos, int) and pos == 0:
+            return remote(rows_sib, rows_out.at[m, core], sb_s.at[pos], sb_r.at[m, pos], sibling)
+        return remote(part.at[pos - 1, other], sib.at[m, pos - 1], sb_s.at[pos], sb_r.at[m, pos], sibling)
 
     def back_item(d, j):
-        dist, rows = BACK[j]
-        return POS[SIGN[d] * dist], (rows if d == 0 else 1 - rows)
+        dist, cols = BACK[j]
+        return POS[SIGN[d] * dist], (cols if d == 0 else 1 - cols)
 
     def rs_copy(m, d, j):
         pos, r = back_item(d, j)
-        return remote(part.at[pos, core, pl.ds(r * half, half)], inb.at[d, j],
-                      rs_s.at[pos], rs_r.at[d, j], nbr[d])
+        cols = pl.ds(r * half, half)
+        if j == 0:
+            return remote(rows_out.at[m, :, :, cols], rows_in.at[d], rs_s.at[pos], rs_r.at[d, j], nbr[d])
+        return remote(part.at[pos - 1, core, :, cols], inb.at[d, j - 1], rs_s.at[pos], rs_r.at[d, j], nbr[d])
 
     seen = set()
 
     def need_sib(m, pos):
         if (m, pos) not in seen:
             seen.add((m, pos))
-            sb_copy(m, pos).wait_recv()
+            if pos == 0:
+                landed(rows_out.at[m, other], sb_r.at[m, pos])
+            else:
+                sb_copy(m, pos).wait_recv()
 
     def back(m, j):
         for d in range(2):
             pos, r = back_item(d, j)
             need_sib(m, pos)
-            rows = pl.ds(r * half, half)
-            acc = part[pos, core, rows] + sib[m, pos, rows]
-            if j >= 2:
-                rs_copy(m, d, j - 2).wait_recv()
-                acc = acc + inb[d, j - 2]
-            part[pos, core, rows] = acc
+            if j > 0:
+                cols = pl.ds(r * half, half)
+                acc = part[pos - 1, core, :, cols] + sib[m, pos - 1, :, cols]
+                if j == 2:
+                    rs_copy(m, d, j - 2).wait_recv()
+                    gates = fm[m, d, pl.ds(pl.multiple_of(core * micro, micro), micro)]
+                    sent = jnp.concatenate([rows_in[d, 0], rows_in[d, 1]] * TERMS, axis=0)
+                    acc = acc + dot(gates, sent)
+                elif j > 2:
+                    rs_copy(m, d, j - 2).wait_recv()
+                    acc = acc + inb[d, j - 2 - 1]
+                part[pos - 1, core, :, cols] = acc
             rs_copy(m, d, j).start()
-
-    def st_copy(m, r):
-        rows = pl.ds(m * micro + r * half, half)
-        return pltpu.make_async_copy(outv.at[rows], out_hbm.at[rows], st_sem)
 
     def finish(m, r):
         pos = HERE
         need_sib(m, pos)
-        rows = pl.ds(r * half, half)
-        acc = part[pos, core, rows] + sib[m, pos, rows]
+        cols = pl.ds(r * half, half)
+        acc = part[pos - 1, core, :, cols] + sib[m, pos - 1, :, cols]
         for d in range(2):
-            j = 5 if (r == 1) == (d == 0) else 6
+            j = SENDS - 2 if (r == 1) == (d == 0) else SENDS - 1
             if (m, d, j) not in seen:
                 seen.add((m, d, j))
                 rs_copy(m, d, j).wait_recv()
-            acc = acc + inb[d, j]
-        outv[pl.ds(m * micro + r * half, half)] = acc.astype(BF16)
-        st_copy(m, r).start()
+            acc = acc + inb[d, j - 1]
+        rows = pl.ds(m * micro, micro)
+        outv[rows, cols] = acc.astype(BF16)
+        pltpu.make_async_copy(outv.at[rows, cols], out_hbm.at[rows, cols], st_sem).start()
 
     def combine_send(m, pos):
         combine(m, pos)
@@ -296,9 +340,13 @@
             combine_send(m, pos)
 
     def part_free(m, pos):
-        landed(part.at[pos, other], sb_s.at[pos])
+        if pos == 0:
+            landed(rows_sib, sb_s.at[pos])
+            landed(rows_out.at[m], rs_s.at[pos])
+            return
+        landed(part.at[pos - 1, other], sb_s.at[pos])
         if pos != HERE:
-            landed(part.at[pos, core], rs_s.at[pos])
+            landed(part.at[pos - 1, core], rs_s.at[pos])
 
     def pair_wait(m, p):
         landed(xg.at[m, p, pl.ds(0, chip)], dx_r.at[m, p])
@@ -342,25 +390,33 @@
         gather(m, p)
 
     near, mid, wide, far = 3, 2, 1, 0
-    for k in range(last - 1):
-        mt_event(k)
-        take(0, k * PIECES, (k + 1) * PIECES)
+    mt_event(0)
+    take(0, 0, PIECES)
+    n = PIECES
+    mt_event(1)
+    take(0, n, n + 1)
     prepare(near)
+    take(0, n + 1, n + 2)
+    index(1, near)
+    take(0, n + 2, n + 3)
+    prepare(mid)
+    take(0, n + 3, n + PIECES)
     pair_wait(0, near)
-    mt_event(last - 1)
-    n = (last - 1) * PIECES
+    n += PIECES
+    mt_event(2)
     take(0, n, n + 1)
     gather(0, near)
     take(0, n + 1, n + 2)
     send_own(1, 0, PIECES)
-    index(1, near)
+    index(1, mid)
     take(0, n + 2, n + 3)
-    prepare(mid)
+    prepare(wide)
+    index_far(0, 0)
     take(0, n + 3, n + PIECES)
     fetch(0, mid)
-    n = last * PIECES
+    n += PIECES
     mt_event(last)
-    prepare(wide)
+    index_far(0, 1)
     take(0, n, n + 1)
     prepare(far)
     take(0, n + 1, n + 2)
@@ -374,7 +430,7 @@
         for n, step in enumerate(steps, first):
             due[divmod(step, STEPS) + (c,)] = functools.partial(take, 1, n, n + 1)
     experts(0, due)
-    combine_send(0, 0)
+    far_rows(0)
     n = (last - 1) * PIECES + 1
     pl.when(core == 0)(functools.partial(take, 1, n, n + 1))
     combine_loop(0, 2, FAR)
@@ -385,7 +441,7 @@
     take(1, last * PIECES, last * PIECES + 2)
     combine_loop(0, FAR + 2, CHIPS)
     combine_send(0, HERE)
-    for p in range(near):
+    for p in (wide, far):
         index(1, p)
     for p in range(PAIRS):
         fetch(1, p)
@@ -395,12 +451,14 @@
             need_sib(0, back_item(d, j)[0])
 
     experts(1, {
-        (0, 2): functools.partial(back, 0, 2),
-        (2, 2): functools.partial(back, 0, 3),
+        (0, 1): functools.partial(back, 0, 2),
+        (2, 0): functools.partial(back, 0, 3),
     })
     part_free(0, 0)
-    combine_send(1, 0)
+    far_rows(1)
     back(0, 4)
+    for d in range(2):
+        index_far(1, d)
     part_free(0, 2)
     part_free(0, 3)
     combine_loop(1, 2, FAR)
@@ -440,10 +498,10 @@
         tokens, dim = act_in.shape
         local_experts, _, ffn = w_gate.shape
         micro = tokens // 2
-        half = micro // 2
         mean_load = micro * expert_ids.shape[1] // (local_experts * group)
         cap = mean_load + mean_load // 2
         slots = 4 * cap
+        rows = local_experts * cap
         dma = pltpu.SemaphoreType.DMA
         scratch = [
             pltpu.VMEM((2, 4, 4 * micro, dim), BF16),
@@ -456,9 +514,13 @@
             pltpu.VMEM((4, local_experts * slots, dim), BF16),
             pltpu.VMEM((2, 4, local_experts * slots, 4 * micro), BF16),
             pltpu.VMEM((2, 4, 4 * micro, 3 * local_experts * slots), BF16),
-            pltpu.VMEM((8, 2, micro, dim), F32),
-            pltpu.VMEM((2, 8, micro, dim), F32),
-            pltpu.VMEM((2, 7, half, dim), F32),
+            pltpu.VMEM((2, 2, 2 * micro, 2 * TERMS * rows), BF16),
+            pltpu.VMEM((2, 2, rows, dim), BF16),
+            pltpu.VMEM((rows, dim), BF16),
+            pltpu.VMEM((2, 2, rows, dim // 2), BF16),
+            pltpu.VMEM((CHIPS - 1, 2, micro, dim), F32),
+            pltpu.VMEM((2, CHIPS - 1, micro, dim), F32),
+            pltpu.VMEM((2, SENDS - 1, micro, dim // 2), F32),
             pltpu.VMEM((tokens, dim), BF16),
             pltpu.VMEM((2, 2, 2, dim, GU_TILE), BF16),
             pltpu.VMEM((2, ffn, dim), BF16),

time: 133 us -> 130 us (0.977)
  Pallas kernels: 131 us -> 128 us
    pallas_call x1, Pallas kernels: 131 us -> 128 us  [device_fn(): pl.pallas_call(functools.partial(layer_kernel, group), out_shape=jax.Shap...]
where the time goes in v4:
time: 130 us
  Pallas kernels  128 us (98%)
  local copies, waits for them, and re-layouts  1.88 us (1%)
    pallas_call x1, Pallas kernels, device_fn(): pl.pallas_call(functools.partial(layer_kernel, group), out_shape=jax.Shap...  128 us

profile of v4, /device:TPU:21, one launch (start us, length us, event | category | flops | bytes accessed | tf_op | source)
XLA Modules:
  0.0 130.3 jit_solution(6633573202008094350)
XLA Ops:
  0.0 128.4 %moe_layer.1 = bf16[128,2048]{1,0:T(8,128)(2,1)} custom-call(s32[8,128]{1,0:T(8,128)} %bitcast.3, bf16[64,2048]{1,0:T(8,128)(2,1)} %bitcast.2, bf16[128,2048]{1,0:T(8,128)(2,1)} %x_hbm.1, bf16[4,2048,1024]{2,1,0:T(8,128)(2,1)} %wg_hbm.1, bf16[4,2048,1024]{2,1,0:T(8,128)(2,1)} %wu_hbm.1, bf16[4,1024,2048]{2,1,0:T(8,128)(2,1)} %wd_hbm.1), custom_call_target="tpu_custom_call" | custom-call | tf_op jit(solution)/shard_map/moe_layer/pallas_call | solution.py:535
  128.4 1.9 %copy.8 = bf16[128,2048]{1,0:T(8,128)(2,1)} copy(bf16[128,2048]{1,0:T(8,128)(2,1)} %moe_layer.1) | data formatting | bytes 1048576

commit v5 on v4

--- a/solution.py
+++ b/solution.py
@@ -34,10 +34,10 @@
     return jnp.dot(a, b, preferred_element_type=F32)
 
 
-def layer_kernel(group, ids_hbm, rw_hbm, x_hbm, wg_hbm, wu_hbm, wd_hbm, out_hbm,
-                 xg, meta, ids_v, rw_v, tp, xe, hid, eo, picks, cm, fm, rows_out, rows_sib, rows_in, part, sib, inb, outv, wgu, wdn,
-                 ag_s, ag_r, dx_s, dx_r, mt_s, mt_r, dm_s, dm_r, rs_s, rs_r, sb_s, sb_r,
-                 gu_sem, dn_sem, ld_sem, st_sem):
+def layer_kernel(group, ids_hbm, rw_hbm, x_hbm, wg_hbm, wu_hbm, wd_hbm, outv,
+                 xg, meta, ids_v, rw_v, tp, xe, hid, eo, picks, cm, fm, rows_out, rows_sib, rows_in, part, sib, inb, wgu, wdn,
+                 ag_s, ag_r, dx_s, dx_r, mt_s, mt_r, dm_s, dm_r, rs_s, sb_s, sb_r,
+                 gu_sem, dn_sem, ld_sem):
     micro = outv.shape[0] // 2
     chip = 2 * micro
     dim = outv.shape[1]
@@ -271,10 +271,13 @@
             rows_sib[:, n:n + WIDE] = o[count:]
         sb_copy(m, 0).start()
 
+    def key(pos):
+        return pos if isinstance(pos, int) and pos < 2 else pos // 2 + 1
+
     def sb_copy(m, pos):
         if isinstance(pos, int) and pos == 0:
-            return remote(rows_sib, rows_out.at[m, core], sb_s.at[pos], sb_r.at[m, pos], sibling)
-        return remote(part.at[pos - 1, other], sib.at[m, pos - 1], sb_s.at[pos], sb_r.at[m, pos], sibling)
+            return remote(rows_sib, rows_out.at[m, core], sb_s.at[key(pos)], sb_r.at[m, key(pos)], sibling)
+        return remote(part.at[pos - 1, other], sib.at[m, pos - 1], sb_s.at[key(pos)], sb_r.at[m, key(pos)], sibling)
 
     def back_item(d, j):
         dist, cols = BACK[j]
@@ -284,18 +287,21 @@
         pos, r = back_item(d, j)
         cols = pl.ds(r * half, half)
         if j == 0:
-            return remote(rows_out.at[m, :, :, cols], rows_in.at[d], rs_s.at[pos], rs_r.at[d, j], nbr[d])
-        return remote(part.at[pos - 1, core, :, cols], inb.at[d, j - 1], rs_s.at[pos], rs_r.at[d, j], nbr[d])
+            return remote(rows_out.at[m, :, :, cols], rows_in.at[d], rs_s.at[key(pos)], ag_r.at[d, j // PIECES, j % PIECES], nbr[d])
+        return remote(part.at[pos - 1, core, :, cols], inb.at[d, j - 1], rs_s.at[key(pos)], ag_r.at[d, j // PIECES, j % PIECES], nbr[d])
 
     seen = set()
 
     def need_sib(m, pos):
-        if (m, pos) not in seen:
-            seen.add((m, pos))
+        if (m, key(pos)) not in seen:
+            seen.add((m, key(pos)))
             if pos == 0:
-                landed(rows_out.at[m, other], sb_r.at[m, pos])
+                came = rows_out.at[m, other]
+            elif pos == HERE:
+                came = sib.at[m, 0]
             else:
-                sb_copy(m, pos).wait_recv()
+                came = sib.at[m, pl.ds(pos - pos % 2 - 1, 2)]
+            landed(came, sb_r.at[m, key(pos)])
 
     def back(m, j):
         for d in range(2):
@@ -328,7 +334,6 @@
             acc = acc + inb[d, j - 1]
         rows = pl.ds(m * micro, micro)
         outv[rows, cols] = acc.astype(BF16)
-        pltpu.make_async_copy(outv.at[rows, cols], out_hbm.at[rows, cols], st_sem).start()
 
     def combine_send(m, pos):
         combine(m, pos)
@@ -343,10 +348,11 @@
         if pos == 0:
             landed(rows_sib, sb_s.at[pos])
             landed(rows_out.at[m], rs_s.at[pos])
-            return
-        landed(part.at[pos - 1, other], sb_s.at[pos])
-        if pos != HERE:
-            landed(part.at[pos - 1, core], rs_s.at[pos])
+        elif pos == HERE:
+            landed(part.at[0, other], sb_s.at[pos])
+        else:
+            landed(part.at[pl.ds(pos - 1, 2), other], sb_s.at[key(pos)])
+            landed(part.at[pl.ds(pos - 1, 2), core], rs_s.at[key(pos)])
 
     def pair_wait(m, p):
         landed(xg.at[m, p, pl.ds(0, chip)], dx_r.at[m, p])
@@ -460,7 +466,6 @@
     for d in range(2):
         index_far(1, d)
     part_free(0, 2)
-    part_free(0, 3)
     combine_loop(1, 2, FAR)
     back(0, 5)
     back(0, 6)
@@ -468,7 +473,7 @@
     back(1, 1)
     finish(0, 0)
     finish(0, 1)
-    for pos in (HERE, *range(FAR, CHIPS)):
+    for pos in (HERE, *range(FAR, CHIPS, 2)):
         part_free(0, pos)
     combine_loop(1, FAR, CHIPS)
     combine_send(1, HERE)
@@ -484,9 +489,8 @@
             landed(xg.at[m, pl.ds(0, 2)], dx_s.at[m])
         landed(meta.at[pl.ds(0, 7), 0], mt_s)
         landed(meta.at[pl.ds(0, 8), 0], dm_s)
-        for pos in range(CHIPS):
+        for pos in (0, HERE, *range(2, CHIPS, 2)):
             part_free(1, pos)
-        landed(outv, st_sem)
 
     drain()
 
@@ -521,25 +525,24 @@
             pltpu.VMEM((CHIPS - 1, 2, micro, dim), F32),
             pltpu.VMEM((2, CHIPS - 1, micro, dim), F32),
             pltpu.VMEM((2, SENDS - 1, micro, dim // 2), F32),
-            pltpu.VMEM((tokens, dim), BF16),
             pltpu.VMEM((2, 2, 2, dim, GU_TILE), BF16),
             pltpu.VMEM((2, ffn, dim), BF16),
             dma((2, 2)), dma((2, 4, PIECES)),
             dma((2,)), dma((2, 4)),
             dma, dma((2, 4)),
             dma, dma((4,)),
-            dma((8,)), dma((2, 7)),
-            dma((8,)), dma((2, 8)),
-            dma((2, 2)), dma((2,)), dma((4,)), dma,
+            dma((5,)),
+            dma((5,)), dma((2, 5)),
+            dma((2, 2)), dma((2,)), dma((4,)),
         ]
         return pl.pallas_call(
             functools.partial(layer_kernel, group),
-            out_shape=jax.ShapeDtypeStruct((tokens, dim), BF16),
+            out_shape=pltpu.VMEM((tokens, dim), BF16),
             in_specs=[pl.BlockSpec(memory_space=pl.ANY)] * 6,
-            out_specs=pl.BlockSpec(memory_space=pl.ANY),
+            out_specs=pl.BlockSpec(memory_space=pltpu.VMEM),
             scratch_shapes=scratch,
             compiler_params=pltpu.CompilerParams(collective_id=0, has_side_effects=True,
-                                                 vmem_limit_bytes=67043328),
+                                                 vmem_limit_bytes=66060288),
             name='moe_layer',
         )(expert_ids.T, router_w.T, act_in, w_gate, w_up, w_down)
 

time: 130 us -> 128 us (0.985)
  no operation moved by 1% of the time
where the time goes in v5:
time: 128 us
  Pallas kernels  128 us (100%)
    pallas_call x1, Pallas kernels, device_fn(): pl.pallas_call(functools.partial(layer_kernel, group), out_shape=pltpu.VM...  128 us

profile of v5, /device:TPU:21, one launch (start us, length us, event | category | flops | bytes accessed | tf_op | source)
XLA Modules:
  0.0 128.3 jit_solution(14905969518265980390)
XLA Ops:
  0.0 127.5 %moe_layer.1 = bf16[128,2048]{1,0:T(8,128)(2,1)S(1)} custom-call(s32[8,128]{1,0:T(8,128)} %bitcast.3, bf16[64,2048]{1,0:T(8,128)(2,1)} %bitcast.2, bf16[128,2048]{1,0:T(8,128)(2,1)} %x_hbm.1, bf16[4,2048,1024]{2,1,0:T(8,128)(2,1)} %wg_hbm.1, bf16[4,2048,1024]{2,1,0:T(8,128)(2,1)} %wu_hbm.1, bf16[4,1024,2048]{2,1,0:T(8,128)(2,1)} %wd_hbm.1), custom_call_target="tpu_custom_call" | custom-call | tf_op jit(solution)/shard_map/moe_layer/pallas_call | solution.py:538
  127.5 0.8 copy.8

commit v6 on v5

--- a/solution.py
+++ b/solution.py
@@ -35,8 +35,8 @@
 
 
 def layer_kernel(group, ids_hbm, rw_hbm, x_hbm, wg_hbm, wu_hbm, wd_hbm, outv,
-                 xg, meta, ids_v, rw_v, tp, xe, hid, eo, picks, cm, fm, rows_out, rows_sib, rows_in, part, sib, inb, wgu, wdn,
-                 ag_s, ag_r, dx_s, dx_r, mt_s, mt_r, dm_s, dm_r, rs_s, sb_s, sb_r,
+                 xg, meta, ids_v, xe, hid, eo, picks, cm, fm, rows_out, rows_sib, rows_in, near_out, near_sib, near_in, part, sib, inb, wgu, wdn,
+                 ag_s, ag_r, dx_s, dx_r, mt_s, mt_r, dm_s, dm_r, rs_s, sb_s, sb_r, nr_s, nb_s, nb_r,
                  gu_sem, dn_sem, ld_sem):
     micro = outv.shape[0] // 2
     chip = 2 * micro
@@ -123,8 +123,8 @@
             for d in range(2):
                 dx_copy(m, POS[-SIGN[d] * (k + 1)], core).start()
 
-    def take(m, first, after):
-        for n in range(first, after):
+    def take(m, first, count=1):
+        for n in range(first, first + count):
             ag_event(m, n // PIECES, n % PIECES)
 
     def mt_event(k):
@@ -135,14 +135,15 @@
                     mt_copy(d, k + 1).start()
                 dm_copy(POS[-SIGN[d] * (k + 1)], core).start()
 
+    rw_v = xe.at[local_experts - 1, pl.ds(0, rw_hbm.shape[0])]
+
     def make_meta():
         for m in range(2):
             rows = x_rows(m, HERE, core, 0, micro)
-            tp[m * micro:(m + 1) * micro, 0:rw_v.shape[0]] = lax.dot_general(
-                rows[...], rw_v[...], NT, preferred_element_type=F32)
+            part[0, m, :, 0:rw_v.shape[0]] = lax.dot_general(rows[...], rw_v[...], NT, preferred_element_type=F32)
         ids = ids_v[...].astype(F32)
         expert = lax.broadcasted_iota(jnp.int32, (rw_v.shape[0], chip), 0).astype(F32)
-        logits = tp[...].T[0:rw_v.shape[0]]
+        logits = jnp.concatenate([part[0, m, :, 0:chip] for m in range(2)], axis=0).T[0:rw_v.shape[0]]
         picked = []
         for j in range(8):
             picked.append(jnp.sum(jnp.where(expert == ids[j:j + 1], logits, 0.0), axis=0, keepdims=True))
@@ -166,7 +167,7 @@
 
     def places(info, first, count):
         token = info.shape[1]
-        ids, gates = info[0:8], info[8:16]
+        ids, gates = jnp.split(info, 2)
         chosen, weight = [], []
         for e in range(count):
             hit = ids == (first + e).astype(F32)
@@ -190,13 +191,13 @@
         slot = grid((slots, 2 * chip), 0) - grid((slots, 2 * chip), 1) // micro * cap
         slot = slot.astype(F32)
         at = [slot == place[e] for e in range(local_experts)]
-        picks[m, p] = jnp.concatenate([jnp.where(a, 1.0, 0.0) for a in at], axis=0).astype(BF16)
+        picks[p] = jnp.concatenate([jnp.where(a, 1.0, 0.0) for a in at], axis=0).astype(BF16)
         mix = jnp.concatenate([jnp.where(at[e], weight[e], 0.0) for e in range(local_experts)], axis=0)
         cm[m, p] = lax.dot_general(eye, three_terms(mix), NT, preferred_element_type=F32).astype(BF16)
 
-    def index_far(m, d):
+    def index_far(m, d, step):
         count = 2 * local_experts
-        home = POS[SIGN[d] * (FAR - 1)]
+        home = POS[SIGN[d] * (FAR - 1 - step)]
         first = lax.rem(me - core + group - 2 * SIGN[d], group) * local_experts
         place, weight, eye = places(chip_info(home, m), first, count)
         slot = grid((16, chip), 0).astype(F32)
@@ -205,11 +206,11 @@
         wide, tight = 16 * count, cap * count
         row, col = grid((TERMS * wide, TERMS * tight), 0), grid((TERMS * wide, TERMS * tight), 1)
         i = col % tight
-        fm[m, d] = dot(turned, one((row // wide == col // tight) & (row % wide == i // cap * 16 + i % cap))).astype(BF16)
+        fm[step, d] = dot(turned, one((row // wide == col // tight) & (row % wide == i // cap * 16 + i % cap))).astype(BF16)
 
     def gather(m, p):
         for n in range(0, dim, WIDE):
-            rows = dot(picks[m, p], xg[m, p, :, n:n + WIDE]).astype(BF16)
+            rows = dot(picks[p], xg[m, p, :, n:n + WIDE]).astype(BF16)
             for e in range(local_experts):
                 xe[e, pl.ds(pl.multiple_of(p * slots, 16), slots), n:n + WIDE] = rows[e * slots:(e + 1) * slots]
 
@@ -247,29 +248,45 @@
                     eo[p, pl.ds(pl.multiple_of(e * slots, 16), slots), c:c + MXU] = o[p * slots:(p + 1) * slots]
             after(2, (dn_copy(nxt),))
 
+    def sum_cols(pos):
+        if isinstance(pos, int) and pos // 2 == 1:
+            first = back_item(1 - pos % 2, 2)[1] * half
+            return first, first + half
+        return 0, dim
+
     def combine(m, pos):
         p, top = pos // 2, (pos % 2) * chip
         if not isinstance(pos, int):
             top = pl.multiple_of(top, chip)
         gates = cm[m, p, pl.ds(top, chip)]
-        for n in range(0, dim, WIDE):
+        first, after = sum_cols(pos)
+        for n in range(first, after, WIDE):
             o = eo[p, :, n:n + WIDE]
             acc = dot(gates, jnp.concatenate([o, o, o], axis=0))
             part[pos - 1, 0, :, n:n + WIDE] = acc[:micro]
             part[pos - 1, 1, :, n:n + WIDE] = acc[micro:]
 
-    def far_rows(m):
+    def raw_rows(pos, first, after, own, sent):
         count = local_experts * cap
         shape = (2 * count, local_experts * slots)
         row, col = grid(shape, 0), grid(shape, 1)
         i = row % count
-        owner = jnp.where(row < count, core, other)
+        owner = jnp.where(row < count, core, other) + pos % 2 * 2
         take_row = one(col == i // cap * slots + owner * cap + i % cap)
-        for n in range(0, dim, WIDE):
-            o = dot(take_row, eo[0, :, n:n + WIDE]).astype(BF16)
-            rows_out[m, core, :, n:n + WIDE] = o[:count]
-            rows_sib[:, n:n + WIDE] = o[count:]
+        for n in range(first, after, WIDE):
+            o = dot(take_row, eo[pos // 2, :, n:n + WIDE]).astype(BF16)
+            own[:, n - first:n - first + WIDE] = o[:count]
+            sent[:, n - first:n - first + WIDE] = o[count:]
+
+    def far_rows(m):
+        raw_rows(0, 0, dim, rows_out.at[m, core], rows_sib)
         sb_copy(m, 0).start()
+
+    def near_rows(m):
+        for d in range(2):
+            pos, r = back_item(d, 1)
+            raw_rows(pos, r * half, r * half + half, near_out.at[m, d, core], near_sib.at[d])
+            remote(near_sib.at[d], near_out.at[m, d, core], nb_s.at[d], nb_r.at[m, d], sibling).start()
 
     def key(pos):
         return pos if isinstance(pos, int) and pos < 2 else pos // 2 + 1
@@ -277,6 +294,11 @@
     def sb_copy(m, pos):
         if isinstance(pos, int) and pos == 0:
             return remote(rows_sib, rows_out.at[m, core], sb_s.at[key(pos)], sb_r.at[m, key(pos)], sibling)
+        if isinstance(pos, int):
+            first, after = sum_cols(pos)
+            cols = pl.ds(first, after - first)
+            return remote(part.at[pos - 1, other, :, cols], sib.at[m, pos - 1, :, cols],
+                          sb_s.at[key(pos)], sb_r.at[m, key(pos)], sibling)
         return remote(part.at[pos - 1, other], sib.at[m, pos - 1], sb_s.at[key(pos)], sb_r.at[m, key(pos)], sibling)
 
     def back_item(d, j):
@@ -288,7 +310,9 @@
         cols = pl.ds(r * half, half)
         if j == 0:
             return remote(rows_out.at[m, :, :, cols], rows_in.at[d], rs_s.at[key(pos)], ag_r.at[d, j // PIECES, j % PIECES], nbr[d])
-        return remote(part.at[pos - 1, core, :, cols], inb.at[d, j - 1], rs_s.at[key(pos)], ag_r.at[d, j // PIECES, j % PIECES], nbr[d])
+        if j == 1:
+            return remote(near_out.at[m, d], near_in.at[d], nr_s, ag_r.at[d, j // PIECES, j % PIECES], nbr[d])
+        return remote(part.at[pos - 1, core, :, cols], inb.at[d, j - 2], rs_s.at[key(pos)], ag_r.at[d, j // PIECES, j % PIECES], nbr[d])
 
     seen = set()
 
@@ -299,6 +323,8 @@
                 came = rows_out.at[m, other]
             elif pos == HERE:
                 came = sib.at[m, 0]
+            elif pos // 2 == 1:
+                came = sib.at[m, 1]
             else:
                 came = sib.at[m, pl.ds(pos - pos % 2 - 1, 2)]
             landed(came, sb_r.at[m, key(pos)])
@@ -306,18 +332,20 @@
     def back(m, j):
         for d in range(2):
             pos, r = back_item(d, j)
-            need_sib(m, pos)
-            if j > 0:
+            if j == 1:
+                landed(near_out.at[m, d, other], nb_r.at[m, d])
+            else:
+                need_sib(m, pos)
+            if j > 1:
                 cols = pl.ds(r * half, half)
                 acc = part[pos - 1, core, :, cols] + sib[m, pos - 1, :, cols]
-                if j == 2:
-                    rs_copy(m, d, j - 2).wait_recv()
-                    gates = fm[m, d, pl.ds(pl.multiple_of(core * micro, micro), micro)]
-                    sent = jnp.concatenate([rows_in[d, 0], rows_in[d, 1]] * TERMS, axis=0)
-                    acc = acc + dot(gates, sent)
-                elif j > 2:
-                    rs_copy(m, d, j - 2).wait_recv()
-                    acc = acc + inb[d, j - 2 - 1]
+                rs_copy(m, d, j - 2).wait_recv()
+                if j < FAR:
+                    gates = fm[j - 2, d, pl.ds(pl.multiple_of(core * micro, micro), micro)]
+                    came = near_in if j == last else rows_in
+                    acc = acc + dot(gates, jnp.concatenate([came[d, 0], came[d, 1]] * TERMS, axis=0))
+                else:
+                    acc = acc + inb[d, j - FAR]
                 part[pos - 1, core, :, cols] = acc
             rs_copy(m, d, j).start()
 
@@ -331,7 +359,7 @@
             if (m, d, j) not in seen:
                 seen.add((m, d, j))
                 rs_copy(m, d, j).wait_recv()
-            acc = acc + inb[d, j - 1]
+            acc = acc + inb[d, j - 2]
         rows = pl.ds(m * micro, micro)
         outv[rows, cols] = acc.astype(BF16)
 
@@ -350,6 +378,12 @@
             landed(rows_out.at[m], rs_s.at[pos])
         elif pos == HERE:
             landed(part.at[0, other], sb_s.at[pos])
+        elif pos // 2 == 1:
+            landed(part.at[1, other], sb_s.at[key(pos)])
+            landed(part.at[1, core], rs_s.at[key(pos)])
+            landed(near_out.at[m], nr_s)
+            for d in range(2):
+                landed(near_sib.at[d], nb_s.at[d])
         else:
             landed(part.at[pl.ds(pos - 1, 2), other], sb_s.at[key(pos)])
             landed(part.at[pl.ds(pos - 1, 2), core], rs_s.at[key(pos)])
@@ -396,58 +430,61 @@
         gather(m, p)
 
     near, mid, wide, far = 3, 2, 1, 0
+    gates_ahead = functools.partial(index_far, 0)
     mt_event(0)
     take(0, 0, PIECES)
     n = PIECES
     mt_event(1)
-    take(0, n, n + 1)
+    take(0, n)
     prepare(near)
-    take(0, n + 1, n + 2)
-    index(1, near)
-    take(0, n + 2, n + 3)
+    take(0, n + 1)
+    take(0, n + 2)
     prepare(mid)
-    take(0, n + 3, n + PIECES)
+    take(0, n + 3)
+    gates_ahead(0, 1)
     pair_wait(0, near)
     n += PIECES
     mt_event(2)
-    take(0, n, n + 1)
+    take(0, n)
     gather(0, near)
-    take(0, n + 1, n + 2)
+    gates_ahead(1, 1)
+    take(0, n + 1)
     send_own(1, 0, PIECES)
-    index(1, mid)
-    take(0, n + 2, n + 3)
+    index(1, near)
+    take(0, n + 2)
     prepare(wide)
-    index_far(0, 0)
-    take(0, n + 3, n + PIECES)
+    gates_ahead(0, 0)
+    take(0, n + 3)
     fetch(0, mid)
     n += PIECES
     mt_event(last)
-    index_far(0, 1)
-    take(0, n, n + 1)
+    gates_ahead(1, 0)
+    take(0, n)
     prepare(far)
-    take(0, n + 1, n + 2)
-    pl.when(core == 1)(functools.partial(take, 1, 0, 1))
+    take(0, n + 1)
+    pl.when(core == 1)(functools.partial(take, 1, 0))
     fetch(0, wide)
     fetch(0, far)
-    pl.when(core == 1)(functools.partial(take, 1, 1, 2))
+    pl.when(core == 1)(functools.partial(take, 1, 1))
 
     due = {}
-    for c, first, steps in ((0, 0, (0, 1, 3, 4, 6, 7, 9, 10, 11)), (1, 2, (0, 2, 3, 4, 6, 7, 8, 10))):
+    for c, first, steps in ((0, 0, (0, 1, 2, 4, 5, 6, 8, 9, 10, 11)), (1, 2, (0, 1, 2, 4, 5, 6, 8, 9))):
         for n, step in enumerate(steps, first):
-            due[divmod(step, STEPS) + (c,)] = functools.partial(take, 1, n, n + 1)
+            due[divmod(step, STEPS) + (c,)] = functools.partial(take, 1, n)
     experts(0, due)
     far_rows(0)
-    n = (last - 1) * PIECES + 1
-    pl.when(core == 0)(functools.partial(take, 1, n, n + 1))
-    combine_loop(0, 2, FAR)
+    near_rows(0)
+    combine_send(0, 2)
     back(0, 0)
-    take(1, n + 1, last * PIECES)
+    combine_send(0, 3)
+    n = (last - 1) * PIECES + 2
+    take(1, n, 2)
     back(0, 1)
     combine_loop(0, FAR, FAR + 2)
-    take(1, last * PIECES, last * PIECES + 2)
+    take(1, last * PIECES, 2)
     combine_loop(0, FAR + 2, CHIPS)
     combine_send(0, HERE)
-    for p in (wide, far):
+    for p in (mid, wide, far):
         index(1, p)
     for p in range(PAIRS):
         fetch(1, p)
@@ -456,17 +493,19 @@
         for d in range(2):
             need_sib(0, back_item(d, j)[0])
 
+    back(0, 2)
     experts(1, {
-        (0, 1): functools.partial(back, 0, 2),
-        (2, 0): functools.partial(back, 0, 3),
+        (1, 0): functools.partial(back, 0, 3),
+        (2, 2): functools.partial(back, 0, 4),
     })
     part_free(0, 0)
     far_rows(1)
-    back(0, 4)
-    for d in range(2):
-        index_far(1, d)
     part_free(0, 2)
-    combine_loop(1, 2, FAR)
+    near_rows(1)
+    for i in range(FAR):
+        index_far(1, i // 2, i % 2)
+    combine_send(1, 2)
+    combine_send(1, 3)
     back(0, 5)
     back(0, 6)
     back(1, 0)
@@ -507,33 +546,36 @@
         slots = 4 * cap
         rows = local_experts * cap
         dma = pltpu.SemaphoreType.DMA
+        both = (2, 2)
         scratch = [
             pltpu.VMEM((2, 4, 4 * micro, dim), BF16),
-            pltpu.VMEM((8, 2, 2, 16, 2 * micro), F32),
+            pltpu.VMEM((CHIPS, *both, 16, 2 * micro), F32),
             pltpu.VMEM(expert_ids.shape[::-1], jnp.int32),
-            pltpu.VMEM(router_w.shape[::-1], BF16),
-            pltpu.VMEM((tokens, 128), F32),
             pltpu.VMEM((local_experts, 4 * slots, dim), BF16),
             pltpu.VMEM((4 * slots, ffn), BF16),
             pltpu.VMEM((4, local_experts * slots, dim), BF16),
-            pltpu.VMEM((2, 4, local_experts * slots, 4 * micro), BF16),
+            pltpu.VMEM((4, local_experts * slots, 4 * micro), BF16),
             pltpu.VMEM((2, 4, 4 * micro, 3 * local_experts * slots), BF16),
-            pltpu.VMEM((2, 2, 2 * micro, 2 * TERMS * rows), BF16),
-            pltpu.VMEM((2, 2, rows, dim), BF16),
+            pltpu.VMEM((*both, 2 * micro, 2 * TERMS * rows), BF16),
+            pltpu.VMEM((*both, rows, dim), BF16),
             pltpu.VMEM((rows, dim), BF16),
-            pltpu.VMEM((2, 2, rows, dim // 2), BF16),
+            pltpu.VMEM((*both, rows, dim // 2), BF16),
+            pltpu.VMEM((*both, 2, rows, dim // 2), BF16),
+            pltpu.VMEM((2, rows, dim // 2), BF16),
+            pltpu.VMEM((*both, rows, dim // 2), BF16),
             pltpu.VMEM((CHIPS - 1, 2, micro, dim), F32),
             pltpu.VMEM((2, CHIPS - 1, micro, dim), F32),
-            pltpu.VMEM((2, SENDS - 1, micro, dim // 2), F32),
-            pltpu.VMEM((2, 2, 2, dim, GU_TILE), BF16),
+            pltpu.VMEM((2, SENDS - 2, micro, dim // 2), F32),
+            pltpu.VMEM((*both, 2, dim, GU_TILE), BF16),
             pltpu.VMEM((2, ffn, dim), BF16),
-            dma((2, 2)), dma((2, 4, PIECES)),
+            dma(both), dma((2, 4, PIECES)),
             dma((2,)), dma((2, 4)),
             dma, dma((2, 4)),
             dma, dma((4,)),
             dma((5,)),
             dma((5,)), dma((2, 5)),
-            dma((2, 2)), dma((2,)), dma((4,)),
+            dma, dma((2,)), dma(both),
+            dma(both), dma((2,)), dma((4,)),
         ]
         return pl.pallas_call(
             functools.partial(layer_kernel, group),
@@ -542,7 +584,7 @@
             out_specs=pl.BlockSpec(memory_space=pltpu.VMEM),
             scratch_shapes=scratch,
             compiler_params=pltpu.CompilerParams(collective_id=0, has_side_effects=True,
-                                                 vmem_limit_bytes=66060288),
+                                                 vmem_limit_bytes=66453504),
             name='moe_layer',
         )(expert_ids.T, router_w.T, act_in, w_gate, w_up, w_down)
 

time: 128 us -> 125 us (0.977)
  Pallas kernels: 128 us -> 124 us
    pallas_call x1, Pallas kernels: 128 us -> 124 us  [device_fn(): pl.pallas_call(functools.partial(layer_kernel, group), out_shape=pltpu.VM...]
where the time goes in v6:
time: 125 us
  Pallas kernels  124 us (99%)
    pallas_call x1, Pallas kernels, device_fn(): pl.pallas_call(functools.partial(layer_kernel, group), out_shape=pltpu.VM...  124 us

profile of v6, /device:TPU:21, one launch (start us, length us, event | category | flops | bytes accessed | tf_op | source)
XLA Modules:
  0.0 125.0 jit_solution(289631851758994103)
XLA Ops:
  0.0 124.2 %moe_layer.1 = bf16[128,2048]{1,0:T(8,128)(2,1)S(1)} custom-call(s32[8,128]{1,0:T(8,128)} %bitcast.3, bf16[64,2048]{1,0:T(8,128)(2,1)} %bitcast.2, bf16[128,2048]{1,0:T(8,128)(2,1)} %x_hbm.1, bf16[4,2048,1024]{2,1,0:T(8,128)(2,1)} %wg_hbm.1, bf16[4,2048,1024]{2,1,0:T(8,128)(2,1)} %wu_hbm.1, bf16[4,1024,2048]{2,1,0:T(8,128)(2,1)} %wd_hbm.1), custom_call_target="tpu_custom_call" | custom-call | tf_op jit(solution)/shard_map/moe_layer/pallas_call | solution.py:580
  124.2 0.8 copy.8

commit v7 on v6

--- a/solution.py
+++ b/solution.py
@@ -474,8 +474,8 @@
     experts(0, due)
     far_rows(0)
     near_rows(0)
+    back(0, 0)
     combine_send(0, 2)
-    back(0, 0)
     combine_send(0, 3)
     n = (last - 1) * PIECES + 2
     take(1, n, 2)

time: 125 us -> 125 us (level)
  no operation moved by 1% of the time
where the time goes in v7:
time: 125 us
  Pallas kernels  124 us (99%)
    pallas_call x1, Pallas kernels, device_fn(): pl.pallas_call(functools.partial(layer_kernel, group), out_shape=pltpu.VM...  124 us

profile of v7, /device:TPU:21, one launch (start us, length us, event | category | flops | bytes accessed | tf_op | source)
XLA Modules:
  0.0 125.0 jit_solution(2805264122698636619)
XLA Ops:
  0.0 124.2 %moe_layer.1 = bf16[128,2048]{1,0:T(8,128)(2,1)S(1)} custom-call(s32[8,128]{1,0:T(8,128)} %bitcast.3, bf16[64,2048]{1,0:T(8,128)(2,1)} %bitcast.2, bf16[128,2048]{1,0:T(8,128)(2,1)} %x_hbm.1, bf16[4,2048,1024]{2,1,0:T(8,128)(2,1)} %wg_hbm.1, bf16[4,2048,1024]{2,1,0:T(8,128)(2,1)} %wu_hbm.1, bf16[4,1024,2048]{2,1,0:T(8,128)(2,1)} %wd_hbm.1), custom_call_target="tpu_custom_call" | custom-call | tf_op jit(solution)/shard_map/moe_layer/pallas_call | solution.py:580
  124.2 0.8 copy.8
